TPU v7x, 512 devices: a whole 4x4x16 slice. The times are simulated.
512 devices in a mesh: gx: 8 (over x, core), gy: 8 (over z_lo), gz: 8 (over z_hi, y).
Axes of the slice: x: 4, y: 4, z: 16 (z_hi: 2, z_lo: 8; z = z_hi * 8 + z_lo), core: 2. Of those that a mesh axis runs over, the one named last changes fastest.
Arguments:
- attn_out: bfloat16 [1408, 8192], P('gx', ('gz', 'gy')), may hold values from -6 to 6
- residual: bfloat16 [1408, 8192], P('gx', ('gy', 'gz')), may hold values from -60 to 60
- proj_weight: bfloat16 [8192, 8192], P(('gz', 'gx'), 'gy'), may hold values from -0.0625 to 0.0625
- norm_gain: float32 [8192], P(('gy', 'gz')), may hold values from 0.1 to 1.9
- gate_proj: bfloat16 [8192, 14336], P(('gy', 'gx'), 'gz'), may hold values from -0.0625 to 0.0625
- up_proj: bfloat16 [8192, 14336], P(('gy', 'gx'), 'gz'), may hold values from -0.0625 to 0.0625
- down_proj: bfloat16 [14336, 8192], P(('gz', 'gx'), 'gy'), may hold values from -0.046875 to 0.046875
Outputs:
- layer_out: bfloat16 [1408, 8192], P('gx', ('gy', 'gz'))
All inputs are finite; a program needn't handle non-finite values.
Results may differ from a plain program's by a relative error of at most 0.0029.
Values may be sent and summed in bfloat16 or wider, within the bound.
No kernel may reach another device: no remote copies, remote signals or barrier semaphores. Data moves between devices by JAX's collectives and lax.ppermute only.
A program may use at most 64 MiB of HBM per device.

v0:
```python
import jax
import jax.numpy as jnp
from jax import lax
from jax.experimental import pallas as pl
from jax.experimental.pallas import tpu as pltpu
from jax.sharding import Mesh
from jax.sharding import PartitionSpec as P


D = 8192
BF = jnp.bfloat16
F32 = jnp.float32
AXES = ("x", "c", "zq", "zp", "zh", "y")
ZL = ("zq", "zp")
TOP = 48


def size_of(axis):
    return lax.axis_size(axis)


def shift(value, axis, step):
    n = size_of(axis)
    return lax.ppermute(value, axis, [(i, (i + step) % n) for i in range(n)])


def swap(value, axis, bit):
    n = size_of(axis)
    return lax.ppermute(value, axis, [(i, i ^ bit) for i in range(n)])


def pick(value, index, dim=0):
    return lax.dynamic_index_in_dim(value, index, dim, keepdims=False)


def exchange(parts, axis):
    return lax.all_to_all(parts, axis, split_axis=0, concat_axis=0, tiled=True)


def from_everyone(value, axis):
    copies = jnp.broadcast_to(value, (size_of(axis), *value.shape))
    return exchange(copies, axis)


def in_bits(own, other, bit):
    first = jnp.where(bit == 0, own, other)
    second = jnp.where(bit == 0, other, own)
    return first, second


def stack_kernel(*refs):
    *ins, out = refs
    height = ins[0].shape[0]
    for k, ref in enumerate(ins):
        out[k * height : (k + 1) * height] = ref[...]


def stacked(parts):
    height, width = parts[0].shape
    vmem = pl.BlockSpec(memory_space=pltpu.VMEM)
    return pl.pallas_call(
        stack_kernel,
        out_shape=jax.ShapeDtypeStruct((len(parts) * height, width), BF),
        in_specs=[vmem] * len(parts),
        out_specs=vmem,
        name="stack",
    )(*parts)


def ring_gathered(w):
    ring = [1, 2, -1]
    shards = [w] + [shift(w, "x", k) for k in ring]
    own = stacked(shards)
    return own, swap(own, "c", 1)


def dot(a, b):
    return jnp.dot(a, b, preferred_element_type=F32)


def proj_kernel(at, first, second, third, fourth, own, other, out, x):
    x[0], x[1], x[2:4], x[4:8] = first[0], second[0], third[...], fourth[...]
    ci, zl = at[0], at[2]
    rows = x.shape[1]

    def blocks(core):
        offs = [(2 * k + core) ^ zl for k in range(4)]
        return [x[((off >> 2) & 1) | (off & 2) | ((off & 1) << 2)] for off in offs]

    mine = jnp.concatenate(blocks(ci), axis=1)
    theirs = jnp.concatenate(blocks(1 - ci), axis=1)
    part = (dot(mine, own[...]) + dot(theirs, other[...])).astype(BF)
    for zh in range(2):
        for y in range(4):
            n = (zh * 4 + y) * 128
            out[y, zh * rows : (zh + 1) * rows] = part[:, n : n + 128]


def proj_parts(at, pieces, own, other):
    rows = pieces[0].shape[1]
    vmem = pl.BlockSpec(memory_space=pltpu.VMEM)
    return pl.pallas_call(
        proj_kernel,
        out_shape=jax.ShapeDtypeStruct((4, 2 * rows, 128), BF),
        in_specs=[pl.BlockSpec(memory_space=pltpu.SMEM)] + [vmem] * 6,
        out_specs=vmem,
        scratch_shapes=[pltpu.VMEM((8, rows, 128), BF)],
        cost_estimate=pl.CostEstimate(
            flops=2 * rows * 1024 * 1024, bytes_accessed=3 << 20, transcendentals=0
        ),
        name="proj_mm",
    )(at, *pieces, own, other)


def both_kernel(at, x, own, other, late_own, late_other, send, keep):
    ci, zp, bit, xi = at[0], at[1], (at[2] >> 1) & 1, at[3]
    rows = (x.shape[1] - 8) // 2

    def blocks(core, steps):
        parts = []
        for k in steps:
            place = (xi + 4 - k) & 3
            row = pl.multiple_of((place >> 1) * rows, 16)
            for turn in range(2):
                at_block = (zp ^ turn) * 4 + (place & 1) * 2 + core
                parts.append(x[at_block, pl.ds(row, rows)])
        return jnp.concatenate(parts, axis=1)

    part = dot(blocks(ci, (0, 2)), own[...]) + dot(blocks(1 - ci, (0, 2)), other[...])
    part += dot(blocks(ci, (1, 3)), late_own[...])
    part += dot(blocks(1 - ci, (1, 3)), late_other[...])
    upper, lower = part[: rows // 2], part[rows // 2 :]
    tile, wide = own.shape[1], send.shape[1] - 128
    cols = pl.ds(pl.multiple_of(pl.program_id(0) * tile, 128), tile)
    send[:, cols] = jnp.where(bit == 0, lower, upper).astype(BF)
    keep[:, cols] = jnp.where(bit == 0, upper, lower)

    @pl.when(pl.program_id(0) == 0)
    def _():
        squares = sum(x[k, pl.ds(2 * rows, 4)].astype(F32) for k in range(8))
        squares = jnp.concatenate([squares[k : k + 1] + squares[k + 2 : k + 3] for k in (0, 1)], 1)
        lane = lax.broadcasted_iota(jnp.int32, (rows // 2, 256), 1)
        row = lax.broadcasted_iota(jnp.int32, (rows // 2, 256), 0)

        def total(half):
            own_lane = jnp.where(lane == row + half * (rows // 2), squares, 0.0)
            return jnp.sum(own_lane, axis=1, keepdims=True)

        send[:, wide:] = in_lanes(total(1 - bit)).astype(BF)
        keep[:, wide:] = in_lanes(total(bit))


def in_lanes(total):
    high = total.astype(BF).astype(F32)
    lane = lax.broadcasted_iota(jnp.int32, (total.shape[0], 128), 1)
    return jnp.where(lane == 0, high, jnp.where(lane == 1, total - high, 0.0))


def both_parts(at, x, weights_of, half):
    depth, wide = weights_of[0].shape
    vmem = pl.BlockSpec(memory_space=pltpu.VMEM)
    weights = pl.BlockSpec((depth, wide // 2), lambda n: (0, n))
    return pl.pallas_call(
        both_kernel,
        grid=(2,),
        out_shape=[jax.ShapeDtypeStruct((half, wide + 128), kind) for kind in (BF, F32)],
        in_specs=[pl.BlockSpec(memory_space=pltpu.SMEM), vmem] + [weights] * 4,
        out_specs=[vmem, vmem],
        cost_estimate=pl.CostEstimate(
            flops=16 * half * depth * wide, bytes_accessed=9 << 20, transcendentals=0
        ),
        name="both_mm",
    )(at, x, *weights_of)


def middle_kernel(at, keep, got, send, rest):
    bit = (at[2] >> 2) & 1
    wide = send.shape[1] - 128
    total = keep[...] + got[...].astype(F32)
    upper, lower = total[:TOP], total[total.shape[0] - TOP :]
    rest[...] = jnp.where(bit == 0, upper, lower)
    sent = jnp.where(bit == 0, lower, upper)
    send[:, :wide] = sent[:, :wide].astype(BF)
    send[:, wide:] = in_lanes(sent[:, wide : wide + 1] + sent[:, wide + 1 : wide + 2]).astype(BF)


def middle(at, keep, got):
    vmem = pl.BlockSpec(memory_space=pltpu.VMEM)
    return pl.pallas_call(
        middle_kernel,
        out_shape=[jax.ShapeDtypeStruct((TOP, keep.shape[1]), kind) for kind in (BF, F32)],
        in_specs=[pl.BlockSpec(memory_space=pltpu.SMEM), vmem, vmem],
        out_specs=[vmem, vmem],
        name="middle",
    )(at, keep, got)


def near_kernel(at, x, own, other, part, rest, whole):
    ci, zp, xi = at[0], at[1], at[3]
    height = own.shape[0] // 4
    half = x.shape[1]
    for ref, core in ((own, ci), (other, 1 - ci)):
        for k in range(4):
            b = ((xi + 4 - k) & 3) * 2 + core
            to = pl.ds(pl.multiple_of(b * height, 16), height)
            whole[to] = ref[k * height : (k + 1) * height]
    part[...] = dot(x[...], whole[pl.ds(pl.multiple_of(zp * half, 16), half)])
    rest[...] = whole[pl.ds(pl.multiple_of((1 - zp) * half, 16), half)]


def far_kernel(x, part, rest, out):
    rows = x.shape[0]
    total = (part[...] + dot(x[...], rest[...])).astype(BF)
    for zh in range(2):
        for y in range(4):
            n = (zh * 4 + y) * 128
            out[y, zh * rows : (zh + 1) * rows] = total[:, n : n + 128]


def near_part(at, x, own, other):
    rows, half = x.shape
    wide = own.shape[1]
    vmem = pl.BlockSpec(memory_space=pltpu.VMEM)
    return pl.pallas_call(
        near_kernel,
        out_shape=(
            jax.ShapeDtypeStruct((rows, wide), F32),
            jax.ShapeDtypeStruct((half, wide), BF),
        ),
        in_specs=[pl.BlockSpec(memory_space=pltpu.SMEM), vmem, vmem, vmem],
        out_specs=(vmem, vmem),
        scratch_shapes=[pltpu.VMEM((2 * half, wide), BF)],
        cost_estimate=pl.CostEstimate(
            flops=2 * rows * half * wide, bytes_accessed=5 << 20, transcendentals=0
        ),
        name="near_mm",
    )(at, x, own, other)


def down_parts(x, part, rest):
    rows, half = x.shape
    vmem = pl.BlockSpec(memory_space=pltpu.VMEM)
    return pl.pallas_call(
        far_kernel,
        out_shape=jax.ShapeDtypeStruct((4, 2 * rows, 128), BF),
        in_specs=[vmem, vmem, vmem],
        out_specs=vmem,
        cost_estimate=pl.CostEstimate(
            flops=2 * rows * half * 1024, bytes_accessed=3 << 20, transcendentals=0
        ),
        name="far_mm",
    )(x, part, rest)


def exact(value):
    return lax.reduce_precision(value, 8, 7)


def on_device(attn_out, residual, proj_weight, norm_gain, gate_proj, up_proj, down_proj):
    xi, ci, zh = (lax.axis_index(name) for name in ("x", "c", "zh"))
    zq, zp = lax.axis_index("zq"), lax.axis_index("zp")
    at = jnp.stack([ci, zp, 2 * zq + zp, xi]).astype(jnp.int32)
    rows = attn_out.shape[0]
    ffw = gate_proj.shape[1] // 2

    cols = attn_out[None]
    pieces = [cols]
    for bit in (4, 2, 1):
        pieces.append(swap(cols, ZL, bit))
        cols = jnp.concatenate(pieces)

    def columns(which):
        halves = [lax.dynamic_slice_in_dim(w, which * ffw, ffw, 1) for w in (gate_proj, up_proj)]
        return jnp.concatenate(halves, axis=1)

    facing = swap(columns(1 - zp), "zp", 1)
    both = jnp.concatenate([columns(zp), facing])
    weights_of = []
    two_hops = shift(both, "x", 2)
    one_hop = [shift(both, "x", 1), shift(both, "x", -1)]
    for shards in ([both, two_hops], one_hop):
        weights_of.append(stacked(shards))
        weights_of.append(swap(weights_of[-1], "c", 1))
    proj_own = from_everyone(proj_weight, "x").reshape(-1, proj_weight.shape[1])
    proj_other = swap(proj_own, "c", 1)
    down_own, down_other = ring_gathered(down_proj)

    high = exact(norm_gain)
    mid = exact(norm_gain - high)
    low = norm_gain - high - mid
    gains = jnp.pad(jnp.stack([high, mid, low]), ((0, 5), (0, 0)))

    part = proj_parts(at, pieces, proj_own, proj_other)
    part, residual = lax.optimization_barrier((part, residual))
    near = exchange(part, "y").astype(F32).sum(axis=0).reshape(2, rows, 128)
    mine = jnp.arange(2)[:, None, None] == zh
    near = jnp.where(mine, near + residual.astype(F32), near).reshape(2 * rows, 128)
    far = swap(jnp.concatenate([near, gains]).astype(BF), "zh", 1).astype(F32)
    stream2 = near + far[: 2 * rows]
    other_gain = far[2 * rows : 2 * rows + 3].sum(axis=0)
    gain2 = jnp.repeat(jnp.stack(in_bits(norm_gain, other_gain, zh)), rows, axis=0)
    squares = jnp.sum((stream2 * stream2).reshape(2, rows, 128), axis=(0, 2))
    scaled2 = (stream2 * gain2).astype(BF)
    squares = jnp.pad(squares, (0, 256 - rows)).reshape(2, 128)
    high = exact(squares)
    tail = jnp.concatenate([high, squares - high, jnp.zeros((4, 128), F32)]).astype(BF)
    model = from_everyone(jnp.concatenate([scaled2, tail]), ("zp", "y"))
    half = rows // 2
    bit1, bit2 = zq & 1, zq >> 1
    send, keep = both_parts(at, model, weights_of, half)
    send, rest = middle(at, keep, swap(send, "zq", 1))
    sums = rest + swap(send, "zq", 2).astype(F32)
    squares = sums[:, 2 * ffw] + sums[:, 2 * ffw + 1]
    inverse = lax.rsqrt(squares / D + 1e-05)[:, None]
    gate_sum, up_sum = inverse * sums[:, :ffw], inverse * sums[:, ffw : 2 * ffw]
    hidden = (jax.nn.silu(gate_sum) * up_sum).astype(BF)
    upper, lower = in_bits(hidden, swap(hidden, "zq", 2), bit2)
    hidden = jnp.concatenate([upper, lower[2 * TOP - half :]])
    hidden = jnp.concatenate(in_bits(hidden, swap(hidden, "zq", 1), bit1))
    hidden, down_other = lax.optimization_barrier((hidden, down_other))
    facing = swap(hidden, "zp", 1)

    part, rest = near_part(at, hidden, down_own, down_other)
    part = down_parts(facing, part, rest)
    near = exchange(part, "y").astype(F32).sum(axis=0).reshape(2, rows, 128)
    far = swap(pick(near, 1 - zh).astype(BF), "zh", 1)
    stream = pick(stream2.reshape(2, rows, 128), zh)
    return (stream + pick(near, zh) + far.astype(F32)).astype(BF)


def solution(mesh):
    z = mesh.shape["gz"] // 4
    split = Mesh(mesh.devices.reshape(4, 2, mesh.shape["gy"] // 2, 2, z, 4), AXES)
    gx, gz = ("x", "c"), ("zh", "y")
    in_specs = (
        P(gx, (*gz, *ZL)),
        P(gx, (*ZL, *gz)),
        P((*gz, *gx), ZL),
        P((*ZL, *gz)),
        P((*ZL, *gx), gz),
        P((*ZL, *gx), gz),
        P((*gz, *gx), ZL),
    )
    return jax.shard_map(
        on_device, mesh=split, in_specs=in_specs, out_specs=P(gx, (*ZL, *gz)), check_vma=False
    )
```

profile of v0, /device:TPU:2, one launch (start us, length us, event | category | flops | bytes accessed | tf_op | source)
XLA Modules:
  0.0 242.7 jit_solution(18079136115687890901)
XLA Ops:
  1.2 18.3 %all_to_all.20 = bf16[4,128,1024]{2,1,0:T(8,128)(2,1)S(1)} all-to-all(bf16[4,128,1024]{2,1,0:T(8,128)(2,1)S(1)} %broadcast_in_dim.34), channel_id=1, replica_groups=mesh['x'=4,'c'=2,'zq'=4,'zp'=2,'zh'=2,'y'=4] {'x'}, dimensions={0} | all-to-all | bytes 2097152 | tf_op jit(solution)/shard_map/all_to_all | solution.py:37
  19.4 1.9 collective-permute-start.3
  21.4 9.1 %collective-permute-start = (bf16[1,176,128]{2,1,0:T(8,128)(2,1)S(1)}, bf16[1,176,128]{2,1,0:T(8,128)(2,1)S(1)}, u32[]{:S(2)}, u32[]{:S(2)}) collective-permute-start(bf16[1,176,128]{2,1,0:T(8,128)(2,1)S(1)} %bitcast.44), channel_id=1, source_target_pairs={{0,32},{8,40},{16,48},{24,56},{32,0},{40,8},{48,16},{56,24},{1,33}... | collective-permute-start | bytes 135176 | tf_op jit(solution)/shard_map/ppermute | solution.py:29
  30.5 2.3 collective-permute-done.second
  33.4 5.5 %collective-permute-start.1 = (bf16[2,176,128]{2,1,0:T(8,128)(2,1)S(1)}, bf16[2,176,128]{2,1,0:T(8,128)(2,1)S(1)}, u32[]{:S(2)}, u32[]{:S(2)}) collective-permute-start(bf16[2,176,128]{2,1,0:T(8,128)(2,1)S(1)} %pad_maximum_fusion.6), channel_id=1, source_target_pairs={{0,16},{8,24},{16,0},{24,8},{32,48},{40,56},{48,32},{56,40},{1,17}... | collective-permute-start | bytes 270344 | tf_op jit(solution)/shard_map/ppermute | solution.py:29
  39.0 4.6 %collective-permute-done.1.third = bf16[2,176,128]{2,1,0:T(8,128)(2,1)S(1)} collective-permute-done((bf16[2,176,128]{2,1,0:T(8,128)(2,1)S(1)}, bf16[2,176,128]{2,1,0:T(8,128)(2,1)S(1)}, u32[]{:S(2)}, u32[]{:S(2)}) %collective-permute-start.1) | collective-permute-done | bytes 90144 | tf_op jit(solution)/shard_map/ppermute | solution.py:29
  44.3 2.6 %collective-permute-start.2 = (bf16[4,176,128]{2,1,0:T(8,128)(2,1)}, bf16[4,176,128]{2,1,0:T(8,128)(2,1)}, u32[]{:S(2)}, u32[]{:S(2)}) collective-permute-start(bf16[4,176,128]{2,1,0:T(8,128)(2,1)} %pad_maximum_fusion.3), channel_id=1, source_target_pairs={{0,8},{8,0},{16,24},{24,16},{32,40},{40,32},{48,56},{56,48},{1,9},... | collective-permute-start | bytes 540680 | tf_op jit(solution)/shard_map/ppermute | solution.py:29
  47.0 3.4 %collective-permute-start.5 = (bf16[128,1792]{1,0:T(8,128)(2,1)S(1)}, bf16[128,1792]{1,0:T(8,128)(2,1)S(1)}, u32[]{:S(2)}, u32[]{:S(2)}) collective-permute-start(bf16[128,1792]{1,0:T(8,128)(2,1)S(1)} %pad_maximum_fusion.1), channel_id=1, source_target_pairs={{0,8},{8,0},{1,9},{9,1},{2,10},{10,2},{3,11},{11,3},{4,12},{12,4},... | collective-permute-start | bytes 1376264 | tf_op jit(solution)/shard_map/ppermute | solution.py:29
  51.0 1.6 collective-permute-done.2.fourth
  53.5 3.1 %proj_mm.1 = bf16[4,352,128]{2,1,0:T(8,128)(2,1)} custom-call(s32[4]{0:T(128)} %pad_add_fusion.at, bf16[1,176,128]{2,1,0:T(8,128)(2,1)} %bitcast.43, bf16[1,176,128]{2,1,0:T(8,128)(2,1)} %copy-done.17, bf16[2,176,128]{2,1,0:T(8,128)(2,1)} %copy-done.20, bf16[4,176,128]{2,1,0:T(8,128)(2,1)} %collective-permute-done.2.fourth, bf16[512,1024]{1,0:T(8,128)(2,1)} %bitcast.39, ...), custom_call_target="tpu_custom_call" | custom-call | flops 369098752 | bytes 3145728 | tf_op jit(solution)/shard_map/proj_mm/pallas_call | solution.py:102
  56.6 4.5 %all-to-all-start.1 = ((bf16[4,352,128]{2,1,0:T(8,128)(2,1)}), bf16[4,352,128]{2,1,0:T(8,128)(2,1)S(1)}, u32[]{:S(2)}, u32[]{:S(2)}) async-start(bf16[4,352,128]{2,1,0:T(8,128)(2,1)} %proj_mm.1), calls=%async_computation.1 | async-start | bytes 720896 | tf_op jit(solution)/shard_map/all_to_all | solution.py:37
  61.4 6.9 %all-to-all-done.1 = bf16[4,352,128]{2,1,0:T(8,128)(2,1)S(1)} async-done(((bf16[4,352,128]{2,1,0:T(8,128)(2,1)}), bf16[4,352,128]{2,1,0:T(8,128)(2,1)S(1)}, u32[]{:S(2)}, u32[]{:S(2)}) %all-to-all-start.1) | async-done | bytes 360480 | tf_op jit(solution)/shard_map/all_to_all | solution.py:37
  68.5 16.1 %collective-permute-start.4 = (bf16[360,128]{1,0:T(8,128)(2,1)S(1)}, bf16[360,128]{1,0:T(8,128)(2,1)S(1)}, u32[]{:S(2)}, u32[]{:S(2)}) collective-permute-start(bf16[360,128]{1,0:T(8,128)(2,1)S(1)} %pad_maximum_fusion.5), channel_id=1, source_target_pairs={{0,4},{4,0},{1,5},{5,1},{2,6},{6,2},{3,7},{7,3},{8,12},{12,8},{9,1... | collective-permute-start | bytes 276488 | tf_op jit(solution)/shard_map/ppermute | solution.py:29
  84.6 3.4 %collective-permute-start.6 = (bf16[256,1792]{1,0:T(8,128)(2,1)S(1)}, bf16[256,1792]{1,0:T(8,128)(2,1)S(1)}, u32[]{:S(2)}, u32[]{:S(2)}) collective-permute-start(bf16[256,1792]{1,0:T(8,128)(2,1)S(1)} %pad_maximum_fusion.refs_0_), channel_id=1, source_target_pairs={{0,256},{128,384},{256,0},{384,128},{1,257},{129,385},{257,1},{385... | collective-permute-start | bytes 2752520 | tf_op jit(solution)/shard_map/ppermute | solution.py:24
  88.0 3.4 %collective-permute-start.8 = (bf16[256,1792]{1,0:T(8,128)(2,1)S(1)}, bf16[256,1792]{1,0:T(8,128)(2,1)}, u32[]{:S(2)}, u32[]{:S(2)}) collective-permute-start(bf16[256,1792]{1,0:T(8,128)(2,1)S(1)} %pad_maximum_fusion.refs_0_), channel_id=1, source_target_pairs={{0,128},{128,256},{256,384},{384,0},{1,129},{129,257},{257,385},{3... | collective-permute-start | bytes 2752520 | tf_op jit(solution)/shard_map/ppermute | solution.py:24
  91.4 2.5 %collective-permute-start.9 = (bf16[256,1792]{1,0:T(8,128)(2,1)S(1)}, bf16[256,1792]{1,0:T(8,128)(2,1)}, u32[]{:S(2)}, u32[]{:S(2)}) collective-permute-start(bf16[256,1792]{1,0:T(8,128)(2,1)S(1)} %pad_maximum_fusion.refs_0_), channel_id=1, source_target_pairs={{0,384},{128,0},{256,128},{384,256},{1,385},{129,1},{257,129},{385... | collective-permute-start | bytes 2752520 | tf_op jit(solution)/shard_map/ppermute | solution.py:24
  96.2 3.5 %all-to-all-start.2 = ((bf16[8,360,128]{2,1,0:T(8,128)(2,1)}), bf16[8,360,128]{2,1,0:T(8,128)(2,1)S(1)}, u32[]{:S(2)}, u32[]{:S(2)}) async-start(bf16[8,360,128]{2,1,0:T(8,128)(2,1)} %broadcast_in_dim.37), calls=%async_computation.2 | async-start | bytes 1474560 | tf_op jit(solution)/shard_map/all_to_all | solution.py:37
  99.7 11.5 %collective-permute-done.6.refs_1_ = bf16[256,1792]{1,0:T(8,128)(2,1)S(1)} collective-permute-done((bf16[256,1792]{1,0:T(8,128)(2,1)S(1)}, bf16[256,1792]{1,0:T(8,128)(2,1)S(1)}, u32[]{:S(2)}, u32[]{:S(2)}) %collective-permute-start.6) | collective-permute-done | bytes 917536 | tf_op jit(solution)/shard_map/ppermute | solution.py:24
  112.2 2.8 %stack.55.own = bf16[512,1792]{1,0:T(8,128)(2,1)} custom-call(bf16[256,1792]{1,0:T(8,128)(2,1)} %copy-done.1, bf16[256,1792]{1,0:T(8,128)(2,1)} %copy-done.9), custom_call_target="tpu_custom_call" | custom-call | tf_op jit(solution)/shard_map/stack/pallas_call | solution.py:61
  115.0 1.9 collective-permute-start.7
  117.0 3.2 %collective-permute-done.8.refs_0_ = bf16[256,1792]{1,0:T(8,128)(2,1)} collective-permute-done((bf16[256,1792]{1,0:T(8,128)(2,1)S(1)}, bf16[256,1792]{1,0:T(8,128)(2,1)}, u32[]{:S(2)}, u32[]{:S(2)}) %collective-permute-start.8) | collective-permute-done | bytes 917536 | tf_op jit(solution)/shard_map/ppermute | solution.py:24
  121.3 2.8 %stack.56.late_own = bf16[512,1792]{1,0:T(8,128)(2,1)} custom-call(bf16[256,1792]{1,0:T(8,128)(2,1)} %collective-permute-done.8.refs_0_, bf16[256,1792]{1,0:T(8,128)(2,1)} %collective-permute-done.9.refs_1_), custom_call_target="tpu_custom_call" | custom-call | tf_op jit(solution)/shard_map/stack/pallas_call | solution.py:61
  124.1 2.0 collective-permute-start.10
  126.2 4.1 %collective-permute-done.10.late_other = bf16[512,1792]{1,0:T(8,128)(2,1)} collective-permute-done((bf16[512,1792]{1,0:T(8,128)(2,1)}, bf16[512,1792]{1,0:T(8,128)(2,1)}, u32[]{:S(2)}, u32[]{:S(2)}) %collective-permute-start.10) | collective-permute-done | bytes 1835040 | tf_op jit(solution)/shard_map/ppermute | solution.py:29
  131.2 5.6 %both_mm.1 = (bf16[88,1920]{1,0:T(8,128)(2,1)}, f32[88,1920]{1,0:T(8,128)}) custom-call(s32[4]{0:T(128)} %pad_add_fusion.at, bf16[8,360,128]{2,1,0:T(8,128)(2,1)} %copy-done.2, bf16[512,1792]{1,0:T(8,128)(2,1)} %stack.55.own, bf16[512,1792]{1,0:T(8,128)(2,1)} %copy-done.4, bf16[512,1792]{1,0:T(8,128)(2,1)} %stack.56.late_own, ...), custom_call_target="tpu_custom_call" | custom-call | flops 1291845632 | bytes 9437184 | tf_op jit(solution)/shard_map/both_mm/pallas_call | solution.py:163
  136.8 2.9 %collective-permute-start.11 = (bf16[88,1920]{1,0:T(8,128)(2,1)}, bf16[88,1920]{1,0:T(8,128)(2,1)S(1)}, u32[]{:S(2)}, u32[]{:S(2)}) collective-permute-start(bf16[88,1920]{1,0:T(8,128)(2,1)} %get-tuple-element.18), channel_id=1, source_target_pairs={{0,16},{16,0},{32,48},{48,32},{1,17},{17,1},{33,49},{49,33},{2,18}... | collective-permute-start | bytes 1013768 | tf_op jit(solution)/shard_map/ppermute | solution.py:29
  139.8 2.5 %collective-permute-start.15 = (bf16[224,1024]{1,0:T(8,128)(2,1)S(1)}, bf16[224,1024]{1,0:T(8,128)(2,1)S(1)}, u32[]{:S(2)}, u32[]{:S(2)}) collective-permute-start(bf16[224,1024]{1,0:T(8,128)(2,1)S(1)} %copy-done.10), channel_id=1, source_target_pairs={{0,128},{128,256},{256,384},{384,0},{1,129},{129,257},{257,385},{3... | collective-permute-start | bytes 1376264 | tf_op jit(solution)/shard_map/ppermute | solution.py:24
  142.3 4.9 %collective-permute-start.16 = (bf16[224,1024]{1,0:T(8,128)(2,1)S(1)}, bf16[224,1024]{1,0:T(8,128)(2,1)S(1)}, u32[]{:S(2)}, u32[]{:S(2)}) collective-permute-start(bf16[224,1024]{1,0:T(8,128)(2,1)S(1)} %copy-done.10), channel_id=1, source_target_pairs={{0,256},{128,384},{256,0},{384,128},{1,257},{129,385},{257,1},{385... | collective-permute-start | bytes 1376264 | tf_op jit(solution)/shard_map/ppermute | solution.py:24
  147.2 2.5 %collective-permute-start.17 = (bf16[224,1024]{1,0:T(8,128)(2,1)S(1)}, bf16[224,1024]{1,0:T(8,128)(2,1)S(1)}, u32[]{:S(2)}, u32[]{:S(2)}) collective-permute-start(bf16[224,1024]{1,0:T(8,128)(2,1)S(1)} %copy-done.10), channel_id=1, source_target_pairs={{0,384},{128,0},{256,128},{384,256},{1,385},{129,1},{257,129},{385... | collective-permute-start | bytes 1376264 | tf_op jit(solution)/shard_map/ppermute | solution.py:24
  149.6 7.4 %collective-permute-done.11.got = bf16[88,1920]{1,0:T(8,128)(2,1)S(1)} collective-permute-done((bf16[88,1920]{1,0:T(8,128)(2,1)}, bf16[88,1920]{1,0:T(8,128)(2,1)S(1)}, u32[]{:S(2)}, u32[]{:S(2)}) %collective-permute-start.11) | collective-permute-done | bytes 337952 | tf_op jit(solution)/shard_map/ppermute | solution.py:29
  157.8 2.2 middle.1
  159.9 4.4 %collective-permute-start.12 = (bf16[48,1920]{1,0:T(8,128)(2,1)}, bf16[48,1920]{1,0:T(8,128)(2,1)S(1)}, u32[]{:S(2)}, u32[]{:S(2)}) collective-permute-start(bf16[48,1920]{1,0:T(8,128)(2,1)} %get-tuple-element.20), channel_id=1, source_target_pairs={{0,32},{16,48},{32,0},{48,16},{1,33},{17,49},{33,1},{49,17},{2,34}... | collective-permute-start | bytes 552968 | tf_op jit(solution)/shard_map/ppermute | solution.py:29
  164.4 3.2 %collective-permute-done.17.refs_3_ = bf16[224,1024]{1,0:T(8,128)(2,1)S(1)} collective-permute-done((bf16[224,1024]{1,0:T(8,128)(2,1)S(1)}, bf16[224,1024]{1,0:T(8,128)(2,1)S(1)}, u32[]{:S(2)}, u32[]{:S(2)}) %collective-permute-start.17) | collective-permute-done | bytes 458784 | tf_op jit(solution)/shard_map/ppermute | solution.py:24
  168.4 2.8 %stack.57.own = bf16[896,1024]{1,0:T(8,128)(2,1)} custom-call(bf16[224,1024]{1,0:T(8,128)(2,1)} %refs_0_.1, bf16[224,1024]{1,0:T(8,128)(2,1)} %copy-done.11, bf16[224,1024]{1,0:T(8,128)(2,1)} %copy-done.12, bf16[224,1024]{1,0:T(8,128)(2,1)} %copy-done.13), custom_call_target="tpu_custom_call" | custom-call | tf_op jit(solution)/shard_map/stack/pallas_call | solution.py:61
  171.2 1.9 collective-permute-start.18
  173.1 10.1 %collective-permute-done.12 = bf16[48,1920]{1,0:T(8,128)(2,1)S(1)} collective-permute-done((bf16[48,1920]{1,0:T(8,128)(2,1)}, bf16[48,1920]{1,0:T(8,128)(2,1)S(1)}, u32[]{:S(2)}, u32[]{:S(2)}) %collective-permute-start.12) | collective-permute-done | bytes 184352 | tf_op jit(solution)/shard_map/ppermute | solution.py:29
  183.6 1.9 collective-permute-start.13
  185.5 8.4 %collective-permute-done.13 = bf16[48,896]{1,0:T(8,128)(2,1)S(1)} collective-permute-done((bf16[48,896]{1,0:T(8,128)(2,1)S(1)}, bf16[48,896]{1,0:T(8,128)(2,1)S(1)}, u32[]{:S(2)}, u32[]{:S(2)}) %collective-permute-start.13) | collective-permute-done | bytes 86048 | tf_op jit(solution)/shard_map/ppermute | solution.py:29
  194.0 1.9 collective-permute-start.14
  196.0 6.6 %collective-permute-done.14 = bf16[88,896]{1,0:T(8,128)(2,1)S(1)} collective-permute-done((bf16[88,896]{1,0:T(8,128)(2,1)S(1)}, bf16[88,896]{1,0:T(8,128)(2,1)S(1)}, u32[]{:S(2)}, u32[]{:S(2)}) %collective-permute-start.14) | collective-permute-done | bytes 157728 | tf_op jit(solution)/shard_map/ppermute | solution.py:29
  202.7 1.9 collective-permute-start.19
  204.6 4.4 %near_mm.1 = (f32[176,1024]{1,0:T(8,128)}, bf16[896,1024]{1,0:T(8,128)(2,1)}) custom-call(s32[4]{0:T(128)} %pad_add_fusion.at, bf16[176,896]{1,0:T(8,128)(2,1)} %copy-done.5, bf16[896,1024]{1,0:T(8,128)(2,1)} %stack.57.own, bf16[896,1024]{1,0:T(8,128)(2,1)} %copy-done.3), custom_call_target="tpu_custom_call" | custom-call | flops 322961408 | bytes 5242880 | tf_op jit(solution)/shard_map/near_mm/pallas_call | solution.py:224
  209.0 3.8 %collective-permute-done.19.x = bf16[176,896]{1,0:T(8,128)(2,1)S(1)} collective-permute-done((bf16[176,896]{1,0:T(8,128)(2,1)S(1)}, bf16[176,896]{1,0:T(8,128)(2,1)S(1)}, u32[]{:S(2)}, u32[]{:S(2)}) %collective-permute-start.19) | collective-permute-done | bytes 315424 | tf_op jit(solution)/shard_map/ppermute | solution.py:29
  213.5 3.1 %far_mm.1 = bf16[4,352,128]{2,1,0:T(8,128)(2,1)} custom-call(bf16[176,896]{1,0:T(8,128)(2,1)} %copy-done.22, f32[176,1024]{1,0:T(8,128)} %get-tuple-element.23.part, bf16[896,1024]{1,0:T(8,128)(2,1)} %get-tuple-element.24.rest), custom_call_target="tpu_custom_call" | custom-call | flops 322961408 | bytes 3145728 | tf_op jit(solution)/shard_map/far_mm/pallas_call | solution.py:243
  216.7 3.5 %all-to-all-start.3 = ((bf16[4,352,128]{2,1,0:T(8,128)(2,1)}), bf16[4,352,128]{2,1,0:T(8,128)(2,1)S(1)}, u32[]{:S(2)}, u32[]{:S(2)}) async-start(bf16[4,352,128]{2,1,0:T(8,128)(2,1)} %far_mm.1), calls=%async_computation.3 | async-start | bytes 720896 | tf_op jit(solution)/shard_map/all_to_all | solution.py:37
  220.1 7.2 %all-to-all-done.3 = bf16[4,352,128]{2,1,0:T(8,128)(2,1)S(1)} async-done(((bf16[4,352,128]{2,1,0:T(8,128)(2,1)}), bf16[4,352,128]{2,1,0:T(8,128)(2,1)S(1)}, u32[]{:S(2)}, u32[]{:S(2)}) %all-to-all-start.3) | async-done | bytes 360480 | tf_op jit(solution)/shard_map/all_to_all | solution.py:37
  227.4 7.7 %collective-permute-start.20 = (bf16[176,128]{1,0:T(8,128)(2,1)S(1)}, bf16[176,128]{1,0:T(8,128)(2,1)S(1)}, u32[]{:S(2)}, u32[]{:S(2)}) collective-permute-start(bf16[176,128]{1,0:T(8,128)(2,1)S(1)} %fusion.5), channel_id=1, source_target_pairs={{0,4},{4,0},{1,5},{5,1},{2,6},{6,2},{3,7},{7,3},{8,12},{12,8},{9,1... | collective-permute-start | bytes 135176 | tf_op jit(solution)/shard_map/ppermute | solution.py:29
  235.0 7.1 %collective-permute-done.20 = bf16[176,128]{1,0:T(8,128)(2,1)S(1)} collective-permute-done((bf16[176,128]{1,0:T(8,128)(2,1)S(1)}, bf16[176,128]{1,0:T(8,128)(2,1)S(1)}, u32[]{:S(2)}, u32[]{:S(2)}) %collective-permute-start.20) | collective-permute-done | bytes 45088 | tf_op jit(solution)/shard_map/ppermute | solution.py:29
  (99 shorter events, 13.7 us)
Async XLA Ops:
  0.0 21.3 %copy-start.16 = (bf16[176,128]{1,0:T(8,128)(2,1)S(1)}, bf16[176,128]{1,0:T(8,128)(2,1)}, u32[]{:S(2)}) copy-start(bf16[176,128]{1,0:T(8,128)(2,1)} %param.7) | copy-start | bytes 135172
  0.0 38.9 %copy-start.14 = (bf16[128,1792]{1,0:T(8,128)(2,1)S(1)}, bf16[128,1792]{1,0:T(8,128)(2,1)}, u32[]{:S(2)}) copy-start(bf16[128,1792]{1,0:T(8,128)(2,1)} %param.12) | copy-start | bytes 1376260
  0.0 38.9 %copy-start.15 = (bf16[128,1792]{1,0:T(8,128)(2,1)S(1)}, bf16[128,1792]{1,0:T(8,128)(2,1)}, u32[]{:S(2)}) copy-start(bf16[128,1792]{1,0:T(8,128)(2,1)} %param.11) | copy-start | bytes 1376260
  19.4 33.1 %copy-start = (bf16[4,128,1024]{2,1,0:T(8,128)(2,1)}, bf16[4,128,1024]{2,1,0:T(8,128)(2,1)S(1)}, u32[]{:S(2)}) copy-start(bf16[4,128,1024]{2,1,0:T(8,128)(2,1)S(1)} %all_to_all.20) | copy-start | bytes 3145732
  19.4 33.1 %collective-permute-start.3 = (bf16[512,1024]{1,0:T(8,128)(2,1)S(1)}, bf16[512,1024]{1,0:T(8,128)(2,1)S(1)}, u32[]{:S(2)}, u32[]{:S(2)}) collective-permute-start(bf16[512,1024]{1,0:T(8,128)(2,1)S(1)} %bitcast.38), channel_id=1, source_target_pairs={{0,64},{64,0},{1,65},{65,1},{2,66},{66,2},{3,67},{67,3},{4,68},{68... | collective-permute-start | bytes 3145736 | tf_op jit(solution)/shard_map/ppermute | solution.py:29
  21.4 11.4 %collective-permute-start = (bf16[1,176,128]{2,1,0:T(8,128)(2,1)S(1)}, bf16[1,176,128]{2,1,0:T(8,128)(2,1)S(1)}, u32[]{:S(2)}, u32[]{:S(2)}) collective-permute-start(bf16[1,176,128]{2,1,0:T(8,128)(2,1)S(1)} %bitcast.44), channel_id=1, source_target_pairs={{0,32},{8,40},{16,48},{24,56},{32,0},{40,8},{48,16},{56,24},{1,33}... | collective-permute-start | bytes 135176 | tf_op jit(solution)/shard_map/ppermute | solution.py:29
  33.4 10.2 %collective-permute-start.1 = (bf16[2,176,128]{2,1,0:T(8,128)(2,1)S(1)}, bf16[2,176,128]{2,1,0:T(8,128)(2,1)S(1)}, u32[]{:S(2)}, u32[]{:S(2)}) collective-permute-start(bf16[2,176,128]{2,1,0:T(8,128)(2,1)S(1)} %pad_maximum_fusion.6), channel_id=1, source_target_pairs={{0,16},{8,24},{16,0},{24,8},{32,48},{40,56},{48,32},{56,40},{1,17}... | collective-permute-start | bytes 270344 | tf_op jit(solution)/shard_map/ppermute | solution.py:29
  38.9 4.7 %copy-start.18 = (bf16[1,176,128]{2,1,0:T(8,128)(2,1)S(1)}, bf16[1,176,128]{2,1,0:T(8,128)(2,1)}, u32[]{:S(2)}) copy-start(bf16[1,176,128]{2,1,0:T(8,128)(2,1)} %copy-done.17) | copy-start | bytes 135172
  43.6 3.4 %copy-start.20 = (bf16[2,176,128]{2,1,0:T(8,128)(2,1)}, bf16[2,176,128]{2,1,0:T(8,128)(2,1)S(1)}, u32[]{:S(2)}) copy-start(bf16[2,176,128]{2,1,0:T(8,128)(2,1)S(1)} %collective-permute-done.1.third) | copy-start | bytes 270340
  44.3 8.2 %collective-permute-start.2 = (bf16[4,176,128]{2,1,0:T(8,128)(2,1)}, bf16[4,176,128]{2,1,0:T(8,128)(2,1)}, u32[]{:S(2)}, u32[]{:S(2)}) collective-permute-start(bf16[4,176,128]{2,1,0:T(8,128)(2,1)} %pad_maximum_fusion.3), channel_id=1, source_target_pairs={{0,8},{8,0},{16,24},{24,16},{32,40},{40,32},{48,56},{56,48},{1,9},... | collective-permute-start | bytes 540680 | tf_op jit(solution)/shard_map/ppermute | solution.py:29
  47.0 14.1 %copy-start.24 = (f32[128]{0:T(128)S(1)}, f32[128]{0:T(128)}, u32[]{:S(2)}) copy-start(f32[128]{0:T(128)} %param.10) | copy-start | bytes 1540
  47.0 14.3 %copy-start.23 = (bf16[176,128]{1,0:T(8,128)(2,1)S(1)}, bf16[176,128]{1,0:T(8,128)(2,1)}, u32[]{:S(2)}) copy-start(bf16[176,128]{1,0:T(8,128)(2,1)} %param.8) | copy-start | bytes 135172
  47.0 37.5 %collective-permute-start.5 = (bf16[128,1792]{1,0:T(8,128)(2,1)S(1)}, bf16[128,1792]{1,0:T(8,128)(2,1)S(1)}, u32[]{:S(2)}, u32[]{:S(2)}) collective-permute-start(bf16[128,1792]{1,0:T(8,128)(2,1)S(1)} %pad_maximum_fusion.1), channel_id=1, source_target_pairs={{0,8},{8,0},{1,9},{9,1},{2,10},{10,2},{3,11},{11,3},{4,12},{12,4},... | collective-permute-start | bytes 1376264 | tf_op jit(solution)/shard_map/ppermute | solution.py:29
  52.5 1.0 copy-start.8
  56.6 11.7 %all-to-all-start.1 = ((bf16[4,352,128]{2,1,0:T(8,128)(2,1)}), bf16[4,352,128]{2,1,0:T(8,128)(2,1)S(1)}, u32[]{:S(2)}, u32[]{:S(2)}) async-start(bf16[4,352,128]{2,1,0:T(8,128)(2,1)} %proj_mm.1), calls=%async_computation.1 | async-start | bytes 720896 | tf_op jit(solution)/shard_map/all_to_all | solution.py:37
  68.5 25.4 %collective-permute-start.4 = (bf16[360,128]{1,0:T(8,128)(2,1)S(1)}, bf16[360,128]{1,0:T(8,128)(2,1)S(1)}, u32[]{:S(2)}, u32[]{:S(2)}) collective-permute-start(bf16[360,128]{1,0:T(8,128)(2,1)S(1)} %pad_maximum_fusion.5), channel_id=1, source_target_pairs={{0,4},{4,0},{1,5},{5,1},{2,6},{6,2},{3,7},{7,3},{8,12},{12,8},{9,1... | collective-permute-start | bytes 276488 | tf_op jit(solution)/shard_map/ppermute | solution.py:29
  84.6 11.5 %copy-start.1 = (bf16[256,1792]{1,0:T(8,128)(2,1)}, bf16[256,1792]{1,0:T(8,128)(2,1)S(1)}, u32[]{:S(2)}) copy-start(bf16[256,1792]{1,0:T(8,128)(2,1)S(1)} %pad_maximum_fusion.refs_0_) | copy-start | bytes 2752516
  84.6 26.6 %collective-permute-start.6 = (bf16[256,1792]{1,0:T(8,128)(2,1)S(1)}, bf16[256,1792]{1,0:T(8,128)(2,1)S(1)}, u32[]{:S(2)}, u32[]{:S(2)}) collective-permute-start(bf16[256,1792]{1,0:T(8,128)(2,1)S(1)} %pad_maximum_fusion.refs_0_), channel_id=1, source_target_pairs={{0,256},{128,384},{256,0},{384,128},{1,257},{129,385},{257,1},{385... | collective-permute-start | bytes 2752520 | tf_op jit(solution)/shard_map/ppermute | solution.py:24
  88.0 32.1 %collective-permute-start.8 = (bf16[256,1792]{1,0:T(8,128)(2,1)S(1)}, bf16[256,1792]{1,0:T(8,128)(2,1)}, u32[]{:S(2)}, u32[]{:S(2)}) collective-permute-start(bf16[256,1792]{1,0:T(8,128)(2,1)S(1)} %pad_maximum_fusion.refs_0_), channel_id=1, source_target_pairs={{0,128},{128,256},{256,384},{384,0},{1,129},{129,257},{257,385},{3... | collective-permute-start | bytes 2752520 | tf_op jit(solution)/shard_map/ppermute | solution.py:24
  91.4 29.9 %collective-permute-start.9 = (bf16[256,1792]{1,0:T(8,128)(2,1)S(1)}, bf16[256,1792]{1,0:T(8,128)(2,1)}, u32[]{:S(2)}, u32[]{:S(2)}) collective-permute-start(bf16[256,1792]{1,0:T(8,128)(2,1)S(1)} %pad_maximum_fusion.refs_0_), channel_id=1, source_target_pairs={{0,384},{128,0},{256,128},{384,256},{1,385},{129,1},{257,129},{385... | collective-permute-start | bytes 2752520 | tf_op jit(solution)/shard_map/ppermute | solution.py:24
  94.1 0.7 copy-start.6
  96.2 34.1 %all-to-all-start.2 = ((bf16[8,360,128]{2,1,0:T(8,128)(2,1)}), bf16[8,360,128]{2,1,0:T(8,128)(2,1)S(1)}, u32[]{:S(2)}, u32[]{:S(2)}) async-start(bf16[8,360,128]{2,1,0:T(8,128)(2,1)} %broadcast_in_dim.37), calls=%async_computation.2 | async-start | bytes 1474560 | tf_op jit(solution)/shard_map/all_to_all | solution.py:37
  111.3 1.0 copy-start.9
  115.0 11.2 %collective-permute-start.7 = (bf16[512,1792]{1,0:T(8,128)(2,1)}, bf16[512,1792]{1,0:T(8,128)(2,1)S(1)}, u32[]{:S(2)}, u32[]{:S(2)}) collective-permute-start(bf16[512,1792]{1,0:T(8,128)(2,1)} %stack.55.own), channel_id=1, source_target_pairs={{0,64},{64,0},{1,65},{65,1},{2,66},{66,2},{3,67},{67,3},{4,68},{68... | collective-permute-start | bytes 5505032 | tf_op jit(solution)/shard_map/ppermute | solution.py:29
  124.1 15.6 %copy-start.10 = (bf16[224,1024]{1,0:T(8,128)(2,1)S(1)}, bf16[224,1024]{1,0:T(8,128)(2,1)}, u32[]{:S(2)}) copy-start(bf16[224,1024]{1,0:T(8,128)(2,1)} %refs_0_.1) | copy-start | bytes 1376260
  124.1 6.1 %collective-permute-start.10 = (bf16[512,1792]{1,0:T(8,128)(2,1)}, bf16[512,1792]{1,0:T(8,128)(2,1)}, u32[]{:S(2)}, u32[]{:S(2)}) collective-permute-start(bf16[512,1792]{1,0:T(8,128)(2,1)} %stack.56.late_own), channel_id=1, source_target_pairs={{0,64},{64,0},{1,65},{65,1},{2,66},{66,2},{3,67},{67,3},{4,68},{68... | collective-permute-start | bytes 5505032 | tf_op jit(solution)/shard_map/ppermute | solution.py:29
  126.2 4.1 %copy-start.4 = (bf16[512,1792]{1,0:T(8,128)(2,1)}, bf16[512,1792]{1,0:T(8,128)(2,1)S(1)}, u32[]{:S(2)}) copy-start(bf16[512,1792]{1,0:T(8,128)(2,1)S(1)} %collective-permute-done.7.other) | copy-start | bytes 5505028
  130.3 0.9 copy-start.2
  136.8 20.2 %collective-permute-start.11 = (bf16[88,1920]{1,0:T(8,128)(2,1)}, bf16[88,1920]{1,0:T(8,128)(2,1)S(1)}, u32[]{:S(2)}, u32[]{:S(2)}) collective-permute-start(bf16[88,1920]{1,0:T(8,128)(2,1)} %get-tuple-element.18), channel_id=1, source_target_pairs={{0,16},{16,0},{32,48},{48,32},{1,17},{17,1},{33,49},{49,33},{2,18}... | collective-permute-start | bytes 1013768 | tf_op jit(solution)/shard_map/ppermute | solution.py:29
  139.8 24.6 %collective-permute-start.15 = (bf16[224,1024]{1,0:T(8,128)(2,1)S(1)}, bf16[224,1024]{1,0:T(8,128)(2,1)S(1)}, u32[]{:S(2)}, u32[]{:S(2)}) collective-permute-start(bf16[224,1024]{1,0:T(8,128)(2,1)S(1)} %copy-done.10), channel_id=1, source_target_pairs={{0,128},{128,256},{256,384},{384,0},{1,129},{129,257},{257,385},{3... | collective-permute-start | bytes 1376264 | tf_op jit(solution)/shard_map/ppermute | solution.py:24
  142.3 22.1 %collective-permute-start.16 = (bf16[224,1024]{1,0:T(8,128)(2,1)S(1)}, bf16[224,1024]{1,0:T(8,128)(2,1)S(1)}, u32[]{:S(2)}, u32[]{:S(2)}) collective-permute-start(bf16[224,1024]{1,0:T(8,128)(2,1)S(1)} %copy-done.10), channel_id=1, source_target_pairs={{0,256},{128,384},{256,0},{384,128},{1,257},{129,385},{257,1},{385... | collective-permute-start | bytes 1376264 | tf_op jit(solution)/shard_map/ppermute | solution.py:24
  147.2 20.4 %collective-permute-start.17 = (bf16[224,1024]{1,0:T(8,128)(2,1)S(1)}, bf16[224,1024]{1,0:T(8,128)(2,1)S(1)}, u32[]{:S(2)}, u32[]{:S(2)}) collective-permute-start(bf16[224,1024]{1,0:T(8,128)(2,1)S(1)} %copy-done.10), channel_id=1, source_target_pairs={{0,384},{128,0},{256,128},{384,256},{1,385},{129,1},{257,129},{385... | collective-permute-start | bytes 1376264 | tf_op jit(solution)/shard_map/ppermute | solution.py:24
  157.0 0.7 copy-start.21
  159.9 23.2 %copy-start.19 = (f32[48,1920]{1,0:T(8,128)S(1)}, f32[48,1920]{1,0:T(8,128)}, u32[]{:S(2)}) copy-start(f32[48,1920]{1,0:T(8,128)} %get-tuple-element.19) | copy-start | bytes 1105924
  159.9 23.2 %collective-permute-start.12 = (bf16[48,1920]{1,0:T(8,128)(2,1)}, bf16[48,1920]{1,0:T(8,128)(2,1)S(1)}, u32[]{:S(2)}, u32[]{:S(2)}) collective-permute-start(bf16[48,1920]{1,0:T(8,128)(2,1)} %get-tuple-element.20), channel_id=1, source_target_pairs={{0,32},{16,48},{32,0},{48,16},{1,33},{17,49},{33,1},{49,17},{2,34}... | collective-permute-start | bytes 552968 | tf_op jit(solution)/shard_map/ppermute | solution.py:29
  164.4 3.2 %copy-start.11 = (bf16[224,1024]{1,0:T(8,128)(2,1)}, bf16[224,1024]{1,0:T(8,128)(2,1)S(1)}, u32[]{:S(2)}) copy-start(bf16[224,1024]{1,0:T(8,128)(2,1)S(1)} %collective-permute-done.15.refs_1_) | copy-start | bytes 1376260
  164.4 3.2 %copy-start.12 = (bf16[224,1024]{1,0:T(8,128)(2,1)}, bf16[224,1024]{1,0:T(8,128)(2,1)S(1)}, u32[]{:S(2)}) copy-start(bf16[224,1024]{1,0:T(8,128)(2,1)S(1)} %collective-permute-done.16.refs_2_) | copy-start | bytes 1376260
  167.6 0.8 copy-start.13
  171.2 31.5 %collective-permute-start.18 = (bf16[896,1024]{1,0:T(8,128)(2,1)}, bf16[896,1024]{1,0:T(8,128)(2,1)S(1)}, u32[]{:S(2)}, u32[]{:S(2)}) collective-permute-start(bf16[896,1024]{1,0:T(8,128)(2,1)} %stack.57.own), channel_id=1, source_target_pairs={{0,64},{64,0},{1,65},{65,1},{2,66},{66,2},{3,67},{67,3},{4,68},{68... | collective-permute-start | bytes 5505032 | tf_op jit(solution)/shard_map/ppermute | solution.py:29
  183.6 10.3 %collective-permute-start.13 = (bf16[48,896]{1,0:T(8,128)(2,1)S(1)}, bf16[48,896]{1,0:T(8,128)(2,1)S(1)}, u32[]{:S(2)}, u32[]{:S(2)}) collective-permute-start(bf16[48,896]{1,0:T(8,128)(2,1)S(1)} %fusion.2), channel_id=1, source_target_pairs={{0,32},{16,48},{32,0},{48,16},{1,33},{17,49},{33,1},{49,17},{2,34}... | collective-permute-start | bytes 258056 | tf_op jit(solution)/shard_map/ppermute | solution.py:29
  194.0 8.5 %collective-permute-start.14 = (bf16[88,896]{1,0:T(8,128)(2,1)S(1)}, bf16[88,896]{1,0:T(8,128)(2,1)S(1)}, u32[]{:S(2)}, u32[]{:S(2)}) collective-permute-start(bf16[88,896]{1,0:T(8,128)(2,1)S(1)} %pad_maximum_fusion.4), channel_id=1, source_target_pairs={{0,16},{16,0},{32,48},{48,32},{1,17},{17,1},{33,49},{49,33},{2,18}... | collective-permute-start | bytes 473096 | tf_op jit(solution)/shard_map/ppermute | solution.py:29
  202.6 2.0 copy-start.5
  202.7 2.0 copy-start.3
  202.7 10.1 %collective-permute-start.19 = (bf16[176,896]{1,0:T(8,128)(2,1)S(1)}, bf16[176,896]{1,0:T(8,128)(2,1)S(1)}, u32[]{:S(2)}, u32[]{:S(2)}) collective-permute-start(bf16[176,896]{1,0:T(8,128)(2,1)S(1)} %pad_maximum_fusion.2.x), channel_id=1, source_target_pairs={{0,8},{8,0},{1,9},{9,1},{2,10},{10,2},{3,11},{11,3},{4,12},{12,4},... | collective-permute-start | bytes 946184 | tf_op jit(solution)/shard_map/ppermute | solution.py:29
  212.8 0.7 copy-start.22
  213.5 28.6 %copy-start.7 = (f32[352,128]{1,0:T(8,128)S(1)}, f32[352,128]{1,0:T(8,128)}, u32[]{:S(2)}) copy-start(f32[352,128]{1,0:T(8,128)} %copy-done.6) | copy-start | bytes 540676
  216.7 10.6 %all-to-all-start.3 = ((bf16[4,352,128]{2,1,0:T(8,128)(2,1)}), bf16[4,352,128]{2,1,0:T(8,128)(2,1)S(1)}, u32[]{:S(2)}, u32[]{:S(2)}) async-start(bf16[4,352,128]{2,1,0:T(8,128)(2,1)} %far_mm.1), calls=%async_computation.3 | async-start | bytes 720896 | tf_op jit(solution)/shard_map/all_to_all | solution.py:37
  227.4 14.7 %collective-permute-start.20 = (bf16[176,128]{1,0:T(8,128)(2,1)S(1)}, bf16[176,128]{1,0:T(8,128)(2,1)S(1)}, u32[]{:S(2)}, u32[]{:S(2)}) collective-permute-start(bf16[176,128]{1,0:T(8,128)(2,1)S(1)} %fusion.5), channel_id=1, source_target_pairs={{0,4},{4,0},{1,5},{5,1},{2,6},{6,2},{3,7},{7,3},{8,12},{12,8},{9,1... | collective-permute-start | bytes 135176 | tf_op jit(solution)/shard_map/ppermute | solution.py:29
  (1 other events, 0.6 us)
where the time goes:
time: 244 us; the launch traced here: 243 us
  starting transfers between devices  95.7 us (39%)
  waiting for transfers between devices  88.9 us (36%)
  Pallas kernels  26.8 us (11%)
  blocking collectives  18.3 us (8%)
  local copies, waits for them, and re-layouts  9.07 us (4%)
  other arithmetic  3.37 us (1%)
    ppermute x15, starting transfers between devices, swap(): return lax.ppermute(value, axis, [(i, i ^ bit) for i in range(n)])  65.2 us
    ppermute x15, waiting for transfers between devices, swap(): return lax.ppermute(value, axis, [(i, i ^ bit) for i in range(n)])  55.8 us
    ppermute x6, waiting for transfers between devices, shift(): return lax.ppermute(value, axis, [(i, (i + step) % n) for i in range(n)])  19.1 us
    ppermute x6, starting transfers between devices, shift(): return lax.ppermute(value, axis, [(i, (i + step) % n) for i in range(n)])  19 us
    all_to_all x1, blocking collectives, exchange(): return lax.all_to_all(parts, axis, split_axis=0, concat_axis=0, tiled=True)  18.3 us
    all_to_all x3, waiting for transfers between devices, exchange(): return lax.all_to_all(parts, axis, split_axis=0, concat_axis=0, tiled=True)  14.1 us
    all_to_all x3, starting transfers between devices, exchange(): return lax.all_to_all(parts, axis, split_axis=0, concat_axis=0, tiled=True)  11.5 us
    pallas_call x3, Pallas kernels, stacked(): pl.pallas_call(stack_kernel, out_shape=jax.ShapeDtypeStruct((len(parts) *...  8.44 us
  transfers between devices with their start and end apart: 24, of which 16 were waited for; matrix products, arithmetic and copies ran while one was open for 2% of the time, Pallas kernels for 7%

commit v1 on v0

--- a/solution.py
+++ b/solution.py
@@ -112,13 +112,13 @@
     )(at, *pieces, own, other)
 
 
-def both_kernel(at, x, own, other, late_own, late_other, send, keep):
+def both_kernel(at, x, own, other, send, keep):
     ci, zp, bit, xi = at[0], at[1], (at[2] >> 1) & 1, at[3]
     rows = (x.shape[1] - 8) // 2
 
-    def blocks(core, steps):
+    def blocks(core):
         parts = []
-        for k in steps:
+        for k in range(4):
             place = (xi + 4 - k) & 3
             row = pl.multiple_of((place >> 1) * rows, 16)
             for turn in range(2):
@@ -126,9 +126,7 @@
                 parts.append(x[at_block, pl.ds(row, rows)])
         return jnp.concatenate(parts, axis=1)
 
-    part = dot(blocks(ci, (0, 2)), own[...]) + dot(blocks(1 - ci, (0, 2)), other[...])
-    part += dot(blocks(ci, (1, 3)), late_own[...])
-    part += dot(blocks(1 - ci, (1, 3)), late_other[...])
+    part = dot(blocks(ci), own[...]) + dot(blocks(1 - ci), other[...])
     upper, lower = part[: rows // 2], part[rows // 2 :]
     tile, wide = own.shape[1], send.shape[1] - 128
     cols = pl.ds(pl.multiple_of(pl.program_id(0) * tile, 128), tile)
@@ -156,21 +154,21 @@
     return jnp.where(lane == 0, high, jnp.where(lane == 1, total - high, 0.0))
 
 
-def both_parts(at, x, weights_of, half):
-    depth, wide = weights_of[0].shape
+def both_parts(at, x, own, other, half):
+    depth, wide = own.shape
     vmem = pl.BlockSpec(memory_space=pltpu.VMEM)
     weights = pl.BlockSpec((depth, wide // 2), lambda n: (0, n))
     return pl.pallas_call(
         both_kernel,
         grid=(2,),
         out_shape=[jax.ShapeDtypeStruct((half, wide + 128), kind) for kind in (BF, F32)],
-        in_specs=[pl.BlockSpec(memory_space=pltpu.SMEM), vmem] + [weights] * 4,
+        in_specs=[pl.BlockSpec(memory_space=pltpu.SMEM), vmem, weights, weights],
         out_specs=[vmem, vmem],
         cost_estimate=pl.CostEstimate(
-            flops=16 * half * depth * wide, bytes_accessed=9 << 20, transcendentals=0
+            flops=8 * half * depth * wide, bytes_accessed=9 << 20, transcendentals=0
         ),
         name="both_mm",
-    )(at, x, *weights_of)
+    )(at, x, own, other)
 
 
 def middle_kernel(at, keep, got, send, rest):
@@ -275,12 +273,7 @@
 
     facing = swap(columns(1 - zp), "zp", 1)
     both = jnp.concatenate([columns(zp), facing])
-    weights_of = []
-    two_hops = shift(both, "x", 2)
-    one_hop = [shift(both, "x", 1), shift(both, "x", -1)]
-    for shards in ([both, two_hops], one_hop):
-        weights_of.append(stacked(shards))
-        weights_of.append(swap(weights_of[-1], "c", 1))
+    both_own, both_other = ring_gathered(both)
     proj_own = from_everyone(proj_weight, "x").reshape(-1, proj_weight.shape[1])
     proj_other = swap(proj_own, "c", 1)
     down_own, down_other = ring_gathered(down_proj)
@@ -307,7 +300,7 @@
     model = from_everyone(jnp.concatenate([scaled2, tail]), ("zp", "y"))
     half = rows // 2
     bit1, bit2 = zq & 1, zq >> 1
-    send, keep = both_parts(at, model, weights_of, half)
+    send, keep = both_parts(at, model, both_own, both_other, half)
     send, rest = middle(at, keep, swap(send, "zq", 1))
     sums = rest + swap(send, "zq", 2).astype(F32)
     squares = sums[:, 2 * ffw] + sums[:, 2 * ffw + 1]

time: 244 us -> 240 us (0.984)
  the two profiles are of different devices: /device:TPU:2 before, /device:TPU:6 now
where the time goes in v1:
time: 240 us; the launch traced here: 238 us
  starting transfers between devices  88.6 us (37%)
  waiting for transfers between devices  88.1 us (37%)
  Pallas kernels  25 us (10%)
  blocking collectives  23.7 us (10%)
  local copies, waits for them, and re-layouts  7.98 us (3%)
  other arithmetic  4.52 us (2%)
    ppermute x14, waiting for transfers between devices, swap(): return lax.ppermute(value, axis, [(i, i ^ bit) for i in range(n)])  57 us
    ppermute x14, starting transfers between devices, swap(): return lax.ppermute(value, axis, [(i, i ^ bit) for i in range(n)])  52.7 us
    all_to_all x1, blocking collectives, exchange(): return lax.all_to_all(parts, axis, split_axis=0, concat_axis=0, tiled=True)  23.7 us
    all_to_all x3, starting transfers between devices, exchange(): return lax.all_to_all(parts, axis, split_axis=0, concat_axis=0, tiled=True)  18.9 us
    ppermute x6, waiting for transfers between devices, shift(): return lax.ppermute(value, axis, [(i, (i + step) % n) for i in range(n)])  17.2 us
    ppermute x6, starting transfers between devices, shift(): return lax.ppermute(value, axis, [(i, (i + step) % n) for i in range(n)])  17 us
    all_to_all x3, waiting for transfers between devices, exchange(): return lax.all_to_all(parts, axis, split_axis=0, concat_axis=0, tiled=True)  13.9 us
    pallas_call x2, Pallas kernels, stacked(): pl.pallas_call(stack_kernel, out_shape=jax.ShapeDtypeStruct((len(parts) *...  6.82 us
  transfers between devices with their start and end apart: 23, of which 14 were waited for; matrix products, arithmetic and copies ran while one was open for 2% of the time, Pallas kernels for 7%

profile of v1, /device:TPU:6, one launch (start us, length us, event | category | flops | bytes accessed | tf_op | source)
XLA Modules:
  0.0 238.4 jit_solution(10168408791205456856)
XLA Ops:
  0.0 2.1 broadcast_in_dim.34
  2.1 9.3 %all-to-all-start = ((bf16[4,128,1024]{2,1,0:T(8,128)(2,1)}), bf16[4,128,1024]{2,1,0:T(8,128)(2,1)S(1)}, u32[]{:S(2)}, u32[]{:S(2)}) async-start(bf16[4,128,1024]{2,1,0:T(8,128)(2,1)} %broadcast_in_dim.34), calls=%async_computation | async-start | bytes 2097152 | tf_op jit(solution)/shard_map/all_to_all | solution.py:37
  11.6 1.9 collective-permute-start.5
  13.5 6.7 %all-to-all-done = bf16[4,128,1024]{2,1,0:T(8,128)(2,1)S(1)} async-done(((bf16[4,128,1024]{2,1,0:T(8,128)(2,1)}), bf16[4,128,1024]{2,1,0:T(8,128)(2,1)S(1)}, u32[]{:S(2)}, u32[]{:S(2)}) %all-to-all-start) | async-done | bytes 1048608 | tf_op jit(solution)/shard_map/all_to_all | solution.py:37
  20.3 1.9 collective-permute-start.3
  22.2 8.8 %collective-permute-start = (bf16[1,176,128]{2,1,0:T(8,128)(2,1)S(1)}, bf16[1,176,128]{2,1,0:T(8,128)(2,1)S(1)}, u32[]{:S(2)}, u32[]{:S(2)}) collective-permute-start(bf16[1,176,128]{2,1,0:T(8,128)(2,1)S(1)} %bitcast.44), channel_id=1, source_target_pairs={{0,32},{8,40},{16,48},{24,56},{32,0},{40,8},{48,16},{56,24},{1,33}... | collective-permute-start | bytes 135176 | tf_op jit(solution)/shard_map/ppermute | solution.py:29
  31.7 1.1 pad_maximum_fusion.refs_0_
  32.8 4.0 %collective-permute-start.6 = (bf16[256,1792]{1,0:T(8,128)(2,1)S(1)}, bf16[256,1792]{1,0:T(8,128)(2,1)}, u32[]{:S(2)}, u32[]{:S(2)}) collective-permute-start(bf16[256,1792]{1,0:T(8,128)(2,1)S(1)} %pad_maximum_fusion.refs_0_), channel_id=1, source_target_pairs={{0,128},{128,256},{256,384},{384,0},{1,129},{129,257},{257,385},{3... | collective-permute-start | bytes 2752520 | tf_op jit(solution)/shard_map/ppermute | solution.py:24
  36.8 1.9 collective-permute-start.7
  38.8 3.3 %collective-permute-start.8 = (bf16[256,1792]{1,0:T(8,128)(2,1)S(1)}, bf16[256,1792]{1,0:T(8,128)(2,1)}, u32[]{:S(2)}, u32[]{:S(2)}) collective-permute-start(bf16[256,1792]{1,0:T(8,128)(2,1)S(1)} %pad_maximum_fusion.refs_0_), channel_id=1, source_target_pairs={{0,384},{128,0},{256,128},{384,256},{1,385},{129,1},{257,129},{385... | collective-permute-start | bytes 2752520 | tf_op jit(solution)/shard_map/ppermute | solution.py:24
  42.7 5.2 %collective-permute-start.1 = (bf16[2,176,128]{2,1,0:T(8,128)(2,1)S(1)}, bf16[2,176,128]{2,1,0:T(8,128)(2,1)S(1)}, u32[]{:S(2)}, u32[]{:S(2)}) collective-permute-start(bf16[2,176,128]{2,1,0:T(8,128)(2,1)S(1)} %pad_maximum_fusion.6), channel_id=1, source_target_pairs={{0,16},{8,24},{16,0},{24,8},{32,48},{40,56},{48,32},{56,40},{1,17}... | collective-permute-start | bytes 270344 | tf_op jit(solution)/shard_map/ppermute | solution.py:29
  47.9 4.4 %collective-permute-done.1.third = bf16[2,176,128]{2,1,0:T(8,128)(2,1)S(1)} collective-permute-done((bf16[2,176,128]{2,1,0:T(8,128)(2,1)S(1)}, bf16[2,176,128]{2,1,0:T(8,128)(2,1)S(1)}, u32[]{:S(2)}, u32[]{:S(2)}) %collective-permute-start.1) | collective-permute-done | bytes 90144 | tf_op jit(solution)/shard_map/ppermute | solution.py:29
  53.2 2.3 collective-permute-start.2
  56.2 4.3 %collective-permute-done.2.fourth = bf16[4,176,128]{2,1,0:T(8,128)(2,1)S(1)} collective-permute-done((bf16[4,176,128]{2,1,0:T(8,128)(2,1)S(1)}, bf16[4,176,128]{2,1,0:T(8,128)(2,1)S(1)}, u32[]{:S(2)}, u32[]{:S(2)}) %collective-permute-start.2) | collective-permute-done | bytes 180256 | tf_op jit(solution)/shard_map/ppermute | solution.py:29
  61.3 1.0 copy-done.4
  62.2 3.1 %proj_mm.1 = bf16[4,352,128]{2,1,0:T(8,128)(2,1)} custom-call(s32[4]{0:T(128)} %pad_add_fusion.at, bf16[1,176,128]{2,1,0:T(8,128)(2,1)} %bitcast.43, bf16[1,176,128]{2,1,0:T(8,128)(2,1)} %copy-done.13, bf16[2,176,128]{2,1,0:T(8,128)(2,1)} %copy-done.15, bf16[4,176,128]{2,1,0:T(8,128)(2,1)} %copy-done.18, bf16[512,1024]{1,0:T(8,128)(2,1)} %bitcast.39, ...), custom_call_target="tpu_custom_call" | custom-call | flops 369098752 | bytes 3145728 | tf_op jit(solution)/shard_map/proj_mm/pallas_call | solution.py:102
  65.3 4.5 %all-to-all-start.1 = ((bf16[4,352,128]{2,1,0:T(8,128)(2,1)}), bf16[4,352,128]{2,1,0:T(8,128)(2,1)S(1)}, u32[]{:S(2)}, u32[]{:S(2)}) async-start(bf16[4,352,128]{2,1,0:T(8,128)(2,1)} %proj_mm.1), calls=%async_computation.1 | async-start | bytes 720896 | tf_op jit(solution)/shard_map/all_to_all | solution.py:37
  69.8 6.7 %collective-permute-done.6.refs_1_ = bf16[256,1792]{1,0:T(8,128)(2,1)} collective-permute-done((bf16[256,1792]{1,0:T(8,128)(2,1)S(1)}, bf16[256,1792]{1,0:T(8,128)(2,1)}, u32[]{:S(2)}, u32[]{:S(2)}) %collective-permute-start.6) | collective-permute-done | bytes 917536 | tf_op jit(solution)/shard_map/ppermute | solution.py:24
  76.5 5.7 %collective-permute-done.8.refs_3_ = bf16[256,1792]{1,0:T(8,128)(2,1)} collective-permute-done((bf16[256,1792]{1,0:T(8,128)(2,1)S(1)}, bf16[256,1792]{1,0:T(8,128)(2,1)}, u32[]{:S(2)}, u32[]{:S(2)}) %collective-permute-start.8) | collective-permute-done | bytes 917536 | tf_op jit(solution)/shard_map/ppermute | solution.py:24
  82.2 4.0 %stack.54.own = bf16[1024,1792]{1,0:T(8,128)(2,1)} custom-call(bf16[256,1792]{1,0:T(8,128)(2,1)} %copy-done.1, bf16[256,1792]{1,0:T(8,128)(2,1)} %collective-permute-done.6.refs_1_, bf16[256,1792]{1,0:T(8,128)(2,1)} %collective-permute-done.7.refs_2_, bf16[256,1792]{1,0:T(8,128)(2,1)} %collective-permute-done.8.refs_3_), custom_call_target="tpu_custom_call" | custom-call | tf_op jit(solution)/shard_map/stack/pallas_call | solution.py:61
  86.2 1.9 collective-permute-start.9
  88.4 10.9 %collective-permute-start.4 = (bf16[360,128]{1,0:T(8,128)(2,1)S(1)}, bf16[360,128]{1,0:T(8,128)(2,1)S(1)}, u32[]{:S(2)}, u32[]{:S(2)}) collective-permute-start(bf16[360,128]{1,0:T(8,128)(2,1)S(1)} %pad_maximum_fusion.5), channel_id=1, source_target_pairs={{0,4},{4,0},{1,5},{5,1},{2,6},{6,2},{3,7},{7,3},{8,12},{12,8},{9,1... | collective-permute-start | bytes 276488 | tf_op jit(solution)/shard_map/ppermute | solution.py:29
  99.4 4.8 %collective-permute-done.4 = bf16[360,128]{1,0:T(8,128)(2,1)S(1)} collective-permute-done((bf16[360,128]{1,0:T(8,128)(2,1)S(1)}, bf16[360,128]{1,0:T(8,128)(2,1)S(1)}, u32[]{:S(2)}, u32[]{:S(2)}) %collective-permute-start.4) | collective-permute-done | bytes 92192 | tf_op jit(solution)/shard_map/ppermute | solution.py:29
  104.8 23.7 %all_to_all.20.x = bf16[8,360,128]{2,1,0:T(8,128)(2,1)} all-to-all(bf16[8,360,128]{2,1,0:T(8,128)(2,1)S(1)} %broadcast_in_dim.37), channel_id=1, replica_groups=mesh['x'=4,'c'=2,'zq'=4,'zp'=2,'zh'=2,'y'=4] {'zp','y'}, dimensions={0} | all-to-all | bytes 1474560 | tf_op jit(solution)/shard_map/all_to_all | solution.py:37
  128.5 5.4 %both_mm.1 = (bf16[88,1920]{1,0:T(8,128)(2,1)}, f32[88,1920]{1,0:T(8,128)}) custom-call(s32[4]{0:T(128)} %pad_add_fusion.at, bf16[8,360,128]{2,1,0:T(8,128)(2,1)} %all_to_all.20.x, bf16[1024,1792]{1,0:T(8,128)(2,1)} %stack.54.own, bf16[1024,1792]{1,0:T(8,128)(2,1)} %collective-permute-done.9.other), custom_call_target="tpu_custom_call" | custom-call | flops 1291845632 | bytes 9437184 | tf_op jit(solution)/shard_map/both_mm/pallas_call | solution.py:161
  133.9 1.9 collective-permute-start.10
  135.9 2.5 %collective-permute-start.14 = (bf16[224,1024]{1,0:T(8,128)(2,1)S(1)}, bf16[224,1024]{1,0:T(8,128)(2,1)S(1)}, u32[]{:S(2)}, u32[]{:S(2)}) collective-permute-start(bf16[224,1024]{1,0:T(8,128)(2,1)S(1)} %copy-done.5), channel_id=1, source_target_pairs={{0,128},{128,256},{256,384},{384,0},{1,129},{129,257},{257,385},{3... | collective-permute-start | bytes 1376264 | tf_op jit(solution)/shard_map/ppermute | solution.py:24
  138.4 2.2 collective-permute-start.15
  140.6 3.0 %collective-permute-start.16 = (bf16[224,1024]{1,0:T(8,128)(2,1)S(1)}, bf16[224,1024]{1,0:T(8,128)(2,1)S(1)}, u32[]{:S(2)}, u32[]{:S(2)}) collective-permute-start(bf16[224,1024]{1,0:T(8,128)(2,1)S(1)} %copy-done.5), channel_id=1, source_target_pairs={{0,384},{128,0},{256,128},{384,256},{1,385},{129,1},{257,129},{385... | collective-permute-start | bytes 1376264 | tf_op jit(solution)/shard_map/ppermute | solution.py:24
  143.6 8.3 %collective-permute-done.10.got = bf16[88,1920]{1,0:T(8,128)(2,1)S(1)} collective-permute-done((bf16[88,1920]{1,0:T(8,128)(2,1)}, bf16[88,1920]{1,0:T(8,128)(2,1)S(1)}, u32[]{:S(2)}, u32[]{:S(2)}) %collective-permute-start.10) | collective-permute-done | bytes 337952 | tf_op jit(solution)/shard_map/ppermute | solution.py:29
  152.6 2.2 middle.1
  154.8 2.0 collective-permute-start.11
  156.9 4.8 %collective-permute-done.16.refs_3_ = bf16[224,1024]{1,0:T(8,128)(2,1)S(1)} collective-permute-done((bf16[224,1024]{1,0:T(8,128)(2,1)S(1)}, bf16[224,1024]{1,0:T(8,128)(2,1)S(1)}, u32[]{:S(2)}, u32[]{:S(2)}) %collective-permute-start.16) | collective-permute-done | bytes 458784 | tf_op jit(solution)/shard_map/ppermute | solution.py:24
  162.5 2.8 %stack.55.own = bf16[896,1024]{1,0:T(8,128)(2,1)} custom-call(bf16[224,1024]{1,0:T(8,128)(2,1)} %refs_0_.1, bf16[224,1024]{1,0:T(8,128)(2,1)} %copy-done.6, bf16[224,1024]{1,0:T(8,128)(2,1)} %copy-done.7, bf16[224,1024]{1,0:T(8,128)(2,1)} %copy-done.8), custom_call_target="tpu_custom_call" | custom-call | tf_op jit(solution)/shard_map/stack/pallas_call | solution.py:61
  165.3 1.9 collective-permute-start.17
  167.2 8.9 %collective-permute-done.11 = bf16[48,1920]{1,0:T(8,128)(2,1)S(1)} collective-permute-done((bf16[48,1920]{1,0:T(8,128)(2,1)}, bf16[48,1920]{1,0:T(8,128)(2,1)S(1)}, u32[]{:S(2)}, u32[]{:S(2)}) %collective-permute-start.11) | collective-permute-done | bytes 184352 | tf_op jit(solution)/shard_map/ppermute | solution.py:29
  176.5 1.9 collective-permute-start.12
  178.4 8.4 %collective-permute-done.12 = bf16[48,896]{1,0:T(8,128)(2,1)S(1)} collective-permute-done((bf16[48,896]{1,0:T(8,128)(2,1)S(1)}, bf16[48,896]{1,0:T(8,128)(2,1)S(1)}, u32[]{:S(2)}, u32[]{:S(2)}) %collective-permute-start.12) | collective-permute-done | bytes 86048 | tf_op jit(solution)/shard_map/ppermute | solution.py:29
  187.0 1.9 collective-permute-start.13
  188.9 6.8 %collective-permute-done.13 = bf16[88,896]{1,0:T(8,128)(2,1)S(1)} collective-permute-done((bf16[88,896]{1,0:T(8,128)(2,1)S(1)}, bf16[88,896]{1,0:T(8,128)(2,1)S(1)}, u32[]{:S(2)}, u32[]{:S(2)}) %collective-permute-start.13) | collective-permute-done | bytes 157728 | tf_op jit(solution)/shard_map/ppermute | solution.py:29
  195.9 1.9 collective-permute-start.18
  197.9 4.4 %near_mm.1 = (f32[176,1024]{1,0:T(8,128)}, bf16[896,1024]{1,0:T(8,128)(2,1)}) custom-call(s32[4]{0:T(128)} %pad_add_fusion.at, bf16[176,896]{1,0:T(8,128)(2,1)} %copy-done.3, bf16[896,1024]{1,0:T(8,128)(2,1)} %stack.55.own, bf16[896,1024]{1,0:T(8,128)(2,1)} %copy-done.2), custom_call_target="tpu_custom_call" | custom-call | flops 322961408 | bytes 5242880 | tf_op jit(solution)/shard_map/near_mm/pallas_call | solution.py:222
  202.3 4.0 %collective-permute-done.18.x = bf16[176,896]{1,0:T(8,128)(2,1)S(1)} collective-permute-done((bf16[176,896]{1,0:T(8,128)(2,1)S(1)}, bf16[176,896]{1,0:T(8,128)(2,1)S(1)}, u32[]{:S(2)}, u32[]{:S(2)}) %collective-permute-start.18) | collective-permute-done | bytes 315424 | tf_op jit(solution)/shard_map/ppermute | solution.py:29
  207.0 3.1 %far_mm.1 = bf16[4,352,128]{2,1,0:T(8,128)(2,1)} custom-call(bf16[176,896]{1,0:T(8,128)(2,1)} %copy-done.17, f32[176,1024]{1,0:T(8,128)} %get-tuple-element.23.part, bf16[896,1024]{1,0:T(8,128)(2,1)} %get-tuple-element.24.rest), custom_call_target="tpu_custom_call" | custom-call | flops 322961408 | bytes 3145728 | tf_op jit(solution)/shard_map/far_mm/pallas_call | solution.py:241
  210.1 5.2 %all-to-all-start.3 = ((bf16[4,352,128]{2,1,0:T(8,128)(2,1)}), bf16[4,352,128]{2,1,0:T(8,128)(2,1)S(1)}, u32[]{:S(2)}, u32[]{:S(2)}) async-start(bf16[4,352,128]{2,1,0:T(8,128)(2,1)} %far_mm.1), calls=%async_computation.3 | async-start | bytes 720896 | tf_op jit(solution)/shard_map/all_to_all | solution.py:37
  215.3 7.2 %all-to-all-done.3 = bf16[4,352,128]{2,1,0:T(8,128)(2,1)S(1)} async-done(((bf16[4,352,128]{2,1,0:T(8,128)(2,1)}), bf16[4,352,128]{2,1,0:T(8,128)(2,1)S(1)}, u32[]{:S(2)}, u32[]{:S(2)}) %all-to-all-start.3) | async-done | bytes 360480 | tf_op jit(solution)/shard_map/all_to_all | solution.py:37
  222.6 8.2 %collective-permute-start.19 = (bf16[176,128]{1,0:T(8,128)(2,1)S(1)}, bf16[176,128]{1,0:T(8,128)(2,1)S(1)}, u32[]{:S(2)}, u32[]{:S(2)}) collective-permute-start(bf16[176,128]{1,0:T(8,128)(2,1)S(1)} %fusion.5), channel_id=1, source_target_pairs={{0,4},{4,0},{1,5},{5,1},{2,6},{6,2},{3,7},{7,3},{8,12},{12,8},{9,1... | collective-permute-start | bytes 135176 | tf_op jit(solution)/shard_map/ppermute | solution.py:29
  230.8 7.0 %collective-permute-done.19 = bf16[176,128]{1,0:T(8,128)(2,1)S(1)} collective-permute-done((bf16[176,128]{1,0:T(8,128)(2,1)S(1)}, bf16[176,128]{1,0:T(8,128)(2,1)S(1)}, u32[]{:S(2)}, u32[]{:S(2)}) %collective-permute-start.19) | collective-permute-done | bytes 45088 | tf_op jit(solution)/shard_map/ppermute | solution.py:29
  (88 shorter events, 8.3 us)
Async XLA Ops:
  0.0 11.4 %copy-start.10 = (bf16[128,1792]{1,0:T(8,128)(2,1)S(1)}, bf16[128,1792]{1,0:T(8,128)(2,1)}, u32[]{:S(2)}) copy-start(bf16[128,1792]{1,0:T(8,128)(2,1)} %param.12) | copy-start | bytes 1376260
  0.0 11.4 %copy-start.11 = (bf16[128,1792]{1,0:T(8,128)(2,1)S(1)}, bf16[128,1792]{1,0:T(8,128)(2,1)}, u32[]{:S(2)}) copy-start(bf16[128,1792]{1,0:T(8,128)(2,1)} %param.11) | copy-start | bytes 1376260
  2.1 18.1 %all-to-all-start = ((bf16[4,128,1024]{2,1,0:T(8,128)(2,1)}), bf16[4,128,1024]{2,1,0:T(8,128)(2,1)S(1)}, u32[]{:S(2)}, u32[]{:S(2)}) async-start(bf16[4,128,1024]{2,1,0:T(8,128)(2,1)} %broadcast_in_dim.34), calls=%async_computation | async-start | bytes 2097152 | tf_op jit(solution)/shard_map/all_to_all | solution.py:37
  11.4 10.7 %copy-start.12 = (bf16[176,128]{1,0:T(8,128)(2,1)S(1)}, bf16[176,128]{1,0:T(8,128)(2,1)}, u32[]{:S(2)}) copy-start(bf16[176,128]{1,0:T(8,128)(2,1)} %param.7) | copy-start | bytes 135172
  11.6 19.4 %collective-permute-start.5 = (bf16[128,1792]{1,0:T(8,128)(2,1)S(1)}, bf16[128,1792]{1,0:T(8,128)(2,1)S(1)}, u32[]{:S(2)}, u32[]{:S(2)}) collective-permute-start(bf16[128,1792]{1,0:T(8,128)(2,1)S(1)} %pad_maximum_fusion.1), channel_id=1, source_target_pairs={{0,8},{8,0},{1,9},{9,1},{2,10},{10,2},{3,11},{11,3},{4,12},{12,4},... | collective-permute-start | bytes 1376264 | tf_op jit(solution)/shard_map/ppermute | solution.py:29
  20.3 40.3 %copy-start = (bf16[4,128,1024]{2,1,0:T(8,128)(2,1)}, bf16[4,128,1024]{2,1,0:T(8,128)(2,1)S(1)}, u32[]{:S(2)}) copy-start(bf16[4,128,1024]{2,1,0:T(8,128)(2,1)S(1)} %all-to-all-done) | copy-start | bytes 3145732
  20.3 40.3 %collective-permute-start.3 = (bf16[512,1024]{1,0:T(8,128)(2,1)S(1)}, bf16[512,1024]{1,0:T(8,128)(2,1)S(1)}, u32[]{:S(2)}, u32[]{:S(2)}) collective-permute-start(bf16[512,1024]{1,0:T(8,128)(2,1)S(1)} %bitcast.38), channel_id=1, source_target_pairs={{0,64},{64,0},{1,65},{65,1},{2,66},{66,2},{3,67},{67,3},{4,68},{68... | collective-permute-start | bytes 3145736 | tf_op jit(solution)/shard_map/ppermute | solution.py:29
  22.2 19.9 %collective-permute-start = (bf16[1,176,128]{2,1,0:T(8,128)(2,1)S(1)}, bf16[1,176,128]{2,1,0:T(8,128)(2,1)S(1)}, u32[]{:S(2)}, u32[]{:S(2)}) collective-permute-start(bf16[1,176,128]{2,1,0:T(8,128)(2,1)S(1)} %bitcast.44), channel_id=1, source_target_pairs={{0,32},{8,40},{16,48},{24,56},{32,0},{40,8},{48,16},{56,24},{1,33}... | collective-permute-start | bytes 135176 | tf_op jit(solution)/shard_map/ppermute | solution.py:29
  31.0 0.8 copy-start.9
  32.8 32.5 %copy-start.1 = (bf16[256,1792]{1,0:T(8,128)(2,1)}, bf16[256,1792]{1,0:T(8,128)(2,1)S(1)}, u32[]{:S(2)}) copy-start(bf16[256,1792]{1,0:T(8,128)(2,1)S(1)} %pad_maximum_fusion.refs_0_) | copy-start | bytes 2752516
  32.8 43.6 %collective-permute-start.6 = (bf16[256,1792]{1,0:T(8,128)(2,1)S(1)}, bf16[256,1792]{1,0:T(8,128)(2,1)}, u32[]{:S(2)}, u32[]{:S(2)}) collective-permute-start(bf16[256,1792]{1,0:T(8,128)(2,1)S(1)} %pad_maximum_fusion.refs_0_), channel_id=1, source_target_pairs={{0,128},{128,256},{256,384},{384,0},{1,129},{129,257},{257,385},{3... | collective-permute-start | bytes 2752520 | tf_op jit(solution)/shard_map/ppermute | solution.py:24
  36.8 39.7 %collective-permute-start.7 = (bf16[256,1792]{1,0:T(8,128)(2,1)S(1)}, bf16[256,1792]{1,0:T(8,128)(2,1)}, u32[]{:S(2)}, u32[]{:S(2)}) collective-permute-start(bf16[256,1792]{1,0:T(8,128)(2,1)S(1)} %pad_maximum_fusion.refs_0_), channel_id=1, source_target_pairs={{0,256},{128,384},{256,0},{384,128},{1,257},{129,385},{257,1},{385... | collective-permute-start | bytes 2752520 | tf_op jit(solution)/shard_map/ppermute | solution.py:24
  38.8 43.4 %collective-permute-start.8 = (bf16[256,1792]{1,0:T(8,128)(2,1)S(1)}, bf16[256,1792]{1,0:T(8,128)(2,1)}, u32[]{:S(2)}, u32[]{:S(2)}) collective-permute-start(bf16[256,1792]{1,0:T(8,128)(2,1)S(1)} %pad_maximum_fusion.refs_0_), channel_id=1, source_target_pairs={{0,384},{128,0},{256,128},{384,256},{1,385},{129,1},{257,129},{385... | collective-permute-start | bytes 2752520 | tf_op jit(solution)/shard_map/ppermute | solution.py:24
  42.1 0.6 copy-start.13
  42.7 9.6 %collective-permute-start.1 = (bf16[2,176,128]{2,1,0:T(8,128)(2,1)S(1)}, bf16[2,176,128]{2,1,0:T(8,128)(2,1)S(1)}, u32[]{:S(2)}, u32[]{:S(2)}) collective-permute-start(bf16[2,176,128]{2,1,0:T(8,128)(2,1)S(1)} %pad_maximum_fusion.6), channel_id=1, source_target_pairs={{0,16},{8,24},{16,0},{24,8},{32,48},{40,56},{48,32},{56,40},{1,17}... | collective-permute-start | bytes 270344 | tf_op jit(solution)/shard_map/ppermute | solution.py:29
  52.3 8.3 %copy-start.15 = (bf16[2,176,128]{2,1,0:T(8,128)(2,1)}, bf16[2,176,128]{2,1,0:T(8,128)(2,1)S(1)}, u32[]{:S(2)}) copy-start(bf16[2,176,128]{2,1,0:T(8,128)(2,1)S(1)} %collective-permute-done.1.third) | copy-start | bytes 270340
  53.2 16.6 %copy-start.20 = (f32[128]{0:T(128)S(1)}, f32[128]{0:T(128)}, u32[]{:S(2)}) copy-start(f32[128]{0:T(128)} %param.10) | copy-start | bytes 1540
  53.2 7.4 %collective-permute-start.2 = (bf16[4,176,128]{2,1,0:T(8,128)(2,1)S(1)}, bf16[4,176,128]{2,1,0:T(8,128)(2,1)S(1)}, u32[]{:S(2)}, u32[]{:S(2)}) collective-permute-start(bf16[4,176,128]{2,1,0:T(8,128)(2,1)S(1)} %pad_maximum_fusion.3), channel_id=1, source_target_pairs={{0,8},{8,0},{16,24},{24,16},{32,40},{40,32},{48,56},{56,48},{1,9},... | collective-permute-start | bytes 540680 | tf_op jit(solution)/shard_map/ppermute | solution.py:29
  60.6 0.7 copy-start.18
  61.3 1.0 copy-start.4
  65.3 22.9 %all-to-all-start.1 = ((bf16[4,352,128]{2,1,0:T(8,128)(2,1)}), bf16[4,352,128]{2,1,0:T(8,128)(2,1)S(1)}, u32[]{:S(2)}, u32[]{:S(2)}) async-start(bf16[4,352,128]{2,1,0:T(8,128)(2,1)} %proj_mm.1), calls=%async_computation.1 | async-start | bytes 720896 | tf_op jit(solution)/shard_map/all_to_all | solution.py:37
  69.8 18.3 %copy-start.19 = (bf16[176,128]{1,0:T(8,128)(2,1)S(1)}, bf16[176,128]{1,0:T(8,128)(2,1)}, u32[]{:S(2)}) copy-start(bf16[176,128]{1,0:T(8,128)(2,1)} %param.8) | copy-start | bytes 135172
  86.2 42.3 %collective-permute-start.9 = (bf16[1024,1792]{1,0:T(8,128)(2,1)}, bf16[1024,1792]{1,0:T(8,128)(2,1)}, u32[]{:S(2)}, u32[]{:S(2)}) collective-permute-start(bf16[1024,1792]{1,0:T(8,128)(2,1)} %stack.54.own), channel_id=1, source_target_pairs={{0,64},{64,0},{1,65},{65,1},{2,66},{66,2},{3,67},{67,3},{4,68},{68... | collective-permute-start | bytes 11010056 | tf_op jit(solution)/shard_map/ppermute | solution.py:29
  88.4 15.8 %collective-permute-start.4 = (bf16[360,128]{1,0:T(8,128)(2,1)S(1)}, bf16[360,128]{1,0:T(8,128)(2,1)S(1)}, u32[]{:S(2)}, u32[]{:S(2)}) collective-permute-start(bf16[360,128]{1,0:T(8,128)(2,1)S(1)} %pad_maximum_fusion.5), channel_id=1, source_target_pairs={{0,4},{4,0},{1,5},{5,1},{2,6},{6,2},{3,7},{7,3},{8,12},{12,8},{9,1... | collective-permute-start | bytes 276488 | tf_op jit(solution)/shard_map/ppermute | solution.py:29
  128.5 7.3 %copy-start.5 = (bf16[224,1024]{1,0:T(8,128)(2,1)S(1)}, bf16[224,1024]{1,0:T(8,128)(2,1)}, u32[]{:S(2)}) copy-start(bf16[224,1024]{1,0:T(8,128)(2,1)} %refs_0_.1) | copy-start | bytes 1376260
  133.9 18.0 %collective-permute-start.10 = (bf16[88,1920]{1,0:T(8,128)(2,1)}, bf16[88,1920]{1,0:T(8,128)(2,1)S(1)}, u32[]{:S(2)}, u32[]{:S(2)}) collective-permute-start(bf16[88,1920]{1,0:T(8,128)(2,1)} %get-tuple-element.18), channel_id=1, source_target_pairs={{0,16},{16,0},{32,48},{48,32},{1,17},{17,1},{33,49},{49,33},{2,18}... | collective-permute-start | bytes 1013768 | tf_op jit(solution)/shard_map/ppermute | solution.py:29
  135.9 21.0 %collective-permute-start.14 = (bf16[224,1024]{1,0:T(8,128)(2,1)S(1)}, bf16[224,1024]{1,0:T(8,128)(2,1)S(1)}, u32[]{:S(2)}, u32[]{:S(2)}) collective-permute-start(bf16[224,1024]{1,0:T(8,128)(2,1)S(1)} %copy-done.5), channel_id=1, source_target_pairs={{0,128},{128,256},{256,384},{384,0},{1,129},{129,257},{257,385},{3... | collective-permute-start | bytes 1376264 | tf_op jit(solution)/shard_map/ppermute | solution.py:24
  138.4 18.5 %collective-permute-start.15 = (bf16[224,1024]{1,0:T(8,128)(2,1)S(1)}, bf16[224,1024]{1,0:T(8,128)(2,1)S(1)}, u32[]{:S(2)}, u32[]{:S(2)}) collective-permute-start(bf16[224,1024]{1,0:T(8,128)(2,1)S(1)} %copy-done.5), channel_id=1, source_target_pairs={{0,256},{128,384},{256,0},{384,128},{1,257},{129,385},{257,1},{385... | collective-permute-start | bytes 1376264 | tf_op jit(solution)/shard_map/ppermute | solution.py:24
  140.6 21.1 %collective-permute-start.16 = (bf16[224,1024]{1,0:T(8,128)(2,1)S(1)}, bf16[224,1024]{1,0:T(8,128)(2,1)S(1)}, u32[]{:S(2)}, u32[]{:S(2)}) collective-permute-start(bf16[224,1024]{1,0:T(8,128)(2,1)S(1)} %copy-done.5), channel_id=1, source_target_pairs={{0,384},{128,0},{256,128},{384,256},{1,385},{129,1},{257,129},{385... | collective-permute-start | bytes 1376264 | tf_op jit(solution)/shard_map/ppermute | solution.py:24
  151.9 0.7 copy-start.16
  154.8 21.3 %copy-start.14 = (f32[48,1920]{1,0:T(8,128)S(1)}, f32[48,1920]{1,0:T(8,128)}, u32[]{:S(2)}) copy-start(f32[48,1920]{1,0:T(8,128)} %get-tuple-element.19) | copy-start | bytes 1105924
  154.8 21.3 %collective-permute-start.11 = (bf16[48,1920]{1,0:T(8,128)(2,1)}, bf16[48,1920]{1,0:T(8,128)(2,1)S(1)}, u32[]{:S(2)}, u32[]{:S(2)}) collective-permute-start(bf16[48,1920]{1,0:T(8,128)(2,1)} %get-tuple-element.20), channel_id=1, source_target_pairs={{0,32},{16,48},{32,0},{48,16},{1,33},{17,49},{33,1},{49,17},{2,34}... | collective-permute-start | bytes 552968 | tf_op jit(solution)/shard_map/ppermute | solution.py:29
  156.9 4.8 %copy-start.6 = (bf16[224,1024]{1,0:T(8,128)(2,1)}, bf16[224,1024]{1,0:T(8,128)(2,1)S(1)}, u32[]{:S(2)}) copy-start(bf16[224,1024]{1,0:T(8,128)(2,1)S(1)} %collective-permute-done.14.refs_1_) | copy-start | bytes 1376260
  156.9 4.8 %copy-start.7 = (bf16[224,1024]{1,0:T(8,128)(2,1)}, bf16[224,1024]{1,0:T(8,128)(2,1)S(1)}, u32[]{:S(2)}) copy-start(bf16[224,1024]{1,0:T(8,128)(2,1)S(1)} %collective-permute-done.15.refs_2_) | copy-start | bytes 1376260
  161.7 0.8 copy-start.8
  165.3 30.6 %collective-permute-start.17 = (bf16[896,1024]{1,0:T(8,128)(2,1)}, bf16[896,1024]{1,0:T(8,128)(2,1)S(1)}, u32[]{:S(2)}, u32[]{:S(2)}) collective-permute-start(bf16[896,1024]{1,0:T(8,128)(2,1)} %stack.55.own), channel_id=1, source_target_pairs={{0,64},{64,0},{1,65},{65,1},{2,66},{66,2},{3,67},{67,3},{4,68},{68... | collective-permute-start | bytes 5505032 | tf_op jit(solution)/shard_map/ppermute | solution.py:29
  176.5 10.4 %collective-permute-start.12 = (bf16[48,896]{1,0:T(8,128)(2,1)S(1)}, bf16[48,896]{1,0:T(8,128)(2,1)S(1)}, u32[]{:S(2)}, u32[]{:S(2)}) collective-permute-start(bf16[48,896]{1,0:T(8,128)(2,1)S(1)} %fusion.2), channel_id=1, source_target_pairs={{0,32},{16,48},{32,0},{48,16},{1,33},{17,49},{33,1},{49,17},{2,34}... | collective-permute-start | bytes 258056 | tf_op jit(solution)/shard_map/ppermute | solution.py:29
  187.0 8.8 %collective-permute-start.13 = (bf16[88,896]{1,0:T(8,128)(2,1)S(1)}, bf16[88,896]{1,0:T(8,128)(2,1)S(1)}, u32[]{:S(2)}, u32[]{:S(2)}) collective-permute-start(bf16[88,896]{1,0:T(8,128)(2,1)S(1)} %pad_maximum_fusion.4), channel_id=1, source_target_pairs={{0,16},{16,0},{32,48},{48,32},{1,17},{17,1},{33,49},{49,33},{2,18}... | collective-permute-start | bytes 473096 | tf_op jit(solution)/shard_map/ppermute | solution.py:29
  195.9 2.0 copy-start.3
  195.9 2.0 copy-start.2
  195.9 10.4 %collective-permute-start.18 = (bf16[176,896]{1,0:T(8,128)(2,1)S(1)}, bf16[176,896]{1,0:T(8,128)(2,1)S(1)}, u32[]{:S(2)}, u32[]{:S(2)}) collective-permute-start(bf16[176,896]{1,0:T(8,128)(2,1)S(1)} %pad_maximum_fusion.2.x), channel_id=1, source_target_pairs={{0,8},{8,0},{1,9},{9,1},{2,10},{10,2},{3,11},{11,3},{4,12},{12,4},... | collective-permute-start | bytes 946184 | tf_op jit(solution)/shard_map/ppermute | solution.py:29
  206.3 0.7 copy-start.17
  210.1 12.4 %all-to-all-start.3 = ((bf16[4,352,128]{2,1,0:T(8,128)(2,1)}), bf16[4,352,128]{2,1,0:T(8,128)(2,1)S(1)}, u32[]{:S(2)}, u32[]{:S(2)}) async-start(bf16[4,352,128]{2,1,0:T(8,128)(2,1)} %far_mm.1), calls=%async_computation.3 | async-start | bytes 720896 | tf_op jit(solution)/shard_map/all_to_all | solution.py:37
  222.6 15.2 %collective-permute-start.19 = (bf16[176,128]{1,0:T(8,128)(2,1)S(1)}, bf16[176,128]{1,0:T(8,128)(2,1)S(1)}, u32[]{:S(2)}, u32[]{:S(2)}) collective-permute-start(bf16[176,128]{1,0:T(8,128)(2,1)S(1)} %fusion.5), channel_id=1, source_target_pairs={{0,4},{4,0},{1,5},{5,1},{2,6},{6,2},{3,7},{7,3},{8,12},{12,8},{9,1... | collective-permute-start | bytes 135176 | tf_op jit(solution)/shard_map/ppermute | solution.py:29
